TPU v7x, 128 devices: a whole 4x4x4 slice. The times are simulated.
128 devices in a mesh: tp: 16 (over z, y), dp: 8 (over x, core).
Axes of the slice: x: 4, y: 4, z: 4, core: 2. Of those that a mesh axis runs over, the one named last changes fastest.
Arguments:
- h_main: bfloat16 [8, 512, 2048], P('dp')
- h_mtp: bfloat16 [8, 512, 2048], P('dp')
- labels_main: int32 [8, 512], P('dp')
- labels_mtp: int32 [8, 512], P('dp')
- weight_main: float32 [8, 512], P('dp')
- weight_mtp: float32 [8, 512], P('dp')
- gain_final: float32 [2048], replicated
- gain_mtp: float32 [2048], replicated
- w_out: bfloat16 [2048, 102400], P(None, 'tp')
Outputs:
- output 1: float32 [], replicated
- output 2: bfloat16 [8, 512, 2048], P('dp')
- output 3: bfloat16 [8, 512, 2048], P('dp')
- output 4: float32 [2048, 102400], P('dp', 'tp')
- output 5: float32 [2048], replicated
- output 6: float32 [2048], replicated
All inputs are finite; a program needn't handle non-finite values.
Results may differ from a plain program's by a relative error of at most 0.00844116.
Values sent between devices are 32-bit elements.
A program may use at most 1 GiB of HBM per device.

v0:
```python
import jax
import jax.numpy as jnp
from jax import lax
from jax.sharding import PartitionSpec as P

NORM_EPS = 1e-6
MTP_LAMBDA = 0.3


def solution(mesh):
    def local_step(h_main, h_mtp, labels_main, labels_mtp, weight_main, weight_mtp, gain_final, gain_mtp, w_out):
        batch_loc, seq_len, d_model = h_main.shape
        shard_vocab = w_out.shape[1]
        rows = batch_loc * seq_len
        weight_sums = lax.psum(jnp.stack([jnp.sum(weight_main), jnp.sum(weight_mtp)]), 'dp')
        loss_coefs = jnp.stack([1.0 / weight_sums[0], MTP_LAMBDA / weight_sums[1]])
        row_w = (jnp.stack([weight_main, weight_mtp]).reshape(2, rows) * loss_coefs[:, None]).reshape(2 * rows)
        x_rows = jnp.stack([h_main, h_mtp]).reshape(2, rows, d_model).astype(jnp.float32)
        gain_rows = jnp.stack([gain_final, gain_mtp])[:, None, :]
        inv_rms = lax.rsqrt(jnp.mean(x_rows * x_rows, axis=-1, keepdims=True) + NORM_EPS)
        normed = x_rows * inv_rms
        u_rows = (normed * gain_rows).astype(jnp.bfloat16).reshape(2 * rows, d_model)
        logits = jnp.dot(u_rows, w_out, preferred_element_type=jnp.float32)
        vocab_start = lax.axis_index('tp') * shard_vocab
        local_labels = jnp.stack([labels_main, labels_mtp]).reshape(2 * rows) - vocab_start
        is_target = jnp.arange(shard_vocab, dtype=jnp.int32)[None, :] == local_labels[:, None]
        row_max = lax.pmax(jnp.max(logits, axis=-1), 'tp')
        shifted = jnp.exp(logits - row_max[:, None])
        row_stats = lax.psum(jnp.stack([jnp.sum(shifted, axis=-1), jnp.sum(jnp.where(is_target, logits, 0.0), axis=-1)]), 'tp')
        log_norm = row_max + jnp.log(row_stats[0])
        loss_total = lax.psum(jnp.sum(row_w * (log_norm - row_stats[1])), 'dp')
        soft_probs = shifted * (1.0 / row_stats[0])[:, None]
        grad_z = (row_w[:, None] * jnp.where(is_target, soft_probs - 1.0, soft_probs)).astype(jnp.bfloat16)
        grad_w = lax.dot_general(u_rows, grad_z, (((0,), (0,)), ((), ())), preferred_element_type=jnp.float32)
        grad_w = lax.psum_scatter(grad_w, 'dp', scatter_dimension=0, tiled=True)
        grad_part = lax.dot_general(grad_z, w_out, (((1,), (1,)), ((), ())), preferred_element_type=jnp.float32).astype(jnp.bfloat16)
        grad_u = lax.psum(grad_part.astype(jnp.float32), 'tp').reshape(2, rows, d_model)
        grad_normed = grad_u * gain_rows
        grad_gain = lax.psum(jnp.sum(grad_u * normed, axis=1), 'dp')
        grad_x = inv_rms * (grad_normed - normed * jnp.mean(grad_normed * normed, axis=-1, keepdims=True))
        grad_h = grad_x.astype(jnp.bfloat16).reshape(2, batch_loc, seq_len, d_model)
        return loss_total, grad_h[0], grad_h[1], grad_w, grad_gain[0], grad_gain[1]

    row_spec = P('dp', None)
    return jax.shard_map(local_step, mesh=mesh, in_specs=(P('dp', None, None), P('dp', None, None), row_spec, row_spec, row_spec, row_spec, P(None), P(None), P(None, 'tp')), out_specs=(P(), P('dp', None, None), P('dp', None, None), P('dp', 'tp'), P(None), P(None)), check_vma=False)
```

profile of v0, /device:TPU:1, one launch (start us, length us, event | category | flops | bytes accessed | tf_op | source)
XLA Modules:
  0.0 510.0 jit_solution(4685363805567918986)
XLA Ops:
  8.0 0.0 all-reduce.3.cloned.1.call-start
  8.0 2.7 fusion.6
  10.7 0.6 add_rsqrt_fusion
  11.3 0.0 copy-start.4
  11.3 0.7 pad_maximum_fusion.1
  12.1 0.0 copy-start.2
  12.1 0.0 copy-done.4
  12.1 0.6 copy-done.2
  12.7 2.7 fusion.3
  15.4 0.0 copy-start.1
  15.4 0.0 copy-start.9
  15.4 0.0 copy-start.10
  15.4 35.2 %fusion.11 = (f32[1024]{0:T(1024)S(1)}, f32[1024,6400]{1,0:T(8,128)}) fusion(bf16[1024,2048]{1,0:T(8,128)(2,1)S(1)} %fusion.3, bf16[2048,6400]{1,0:T(8,128)(2,1)} %param.17), kind=kOutput, calls=%fused_computation.36 | convolution fusion | flops 26850099200 | bytes 56627200 | tf_op jit(solution)/shard_map/dot_general | solution.py:23
  50.6 0.0 copy-done.1
  50.6 35.5 %pmax.7 = f32[1024]{0:T(1024)S(1)} all-reduce(f32[1024]{0:T(1024)S(1)} %get-tuple-element.25), channel_id=1, replica_groups=mesh['tp'=16,'dp'=8] {'tp'}, use_global_device_ids=true, to_apply=%region_5.0 | all-reduce | flops 1024 | bytes 8192 | tf_op jit(solution)/shard_map/pmax | solution.py:27
  86.1 0.0 copy-done.9
  86.2 0.0 copy-done.10
  86.2 0.0 copy-start.8
  86.2 0.0 copy-start.7
  86.2 10.4 %fusion.2 = (f32[1024]{0:T(1024)S(1)}, f32[1024]{0:T(1024)S(1)}) fusion(f32[1024,6400]{1,0:T(8,128)} %get-tuple-element.26, f32[1024]{0:T(1024)S(1)} %pmax.7, s32[1024]{0:T(1024)S(1)} %bitcast.68), kind=kLoop, calls=%fused_computation.6 | loop fusion | flops 32765952 | bytes 26230784 | tf_op jit(solution)/shard_map/reduce_sum | solution.py:29
  96.6 29.0 %psum.36 = f32[2,1024]{1,0:T(2,128)S(1)} all-reduce(f32[2,1024]{1,0:T(2,128)S(1)} %pad_maximum_fusion.2), channel_id=1, replica_groups=mesh['tp'=16,'dp'=8] {'tp'}, use_global_device_ids=true, to_apply=%region_8.9 | all-reduce | flops 2048 | bytes 16384 | tf_op jit(solution)/shard_map/psum | solution.py:29
  125.6 0.0 copy-done.8
  125.7 0.6 reduce_sum.72
  126.3 0.0 copy-done.7
  126.3 0.6 reduce_sum.73
  126.9 1.4 pad_maximum_fusion.4
  128.3 26.8 %psum.35 = f32[2]{0:T(128)S(1)} all-reduce(f32[2]{0:T(128)S(1)} %pad_maximum_fusion.4), channel_id=1, replica_groups=mesh['tp'=16,'dp'=8] {'dp'}, use_global_device_ids=true, to_apply=%region_2.0 | all-reduce | flops 2 | bytes 16 | tf_op jit(solution)/shard_map/psum | solution.py:15
  155.1 0.6 fusion.10
  157.0 0.1 pad_maximum_fusion.5
  157.1 0.1 broadcast_bitcast_fusion
  157.2 0.6 multiply_reduce_fusion.1
  157.8 18.3 %fusion.1 = bf16[1024,6400]{1,0:T(8,128)(2,1)} fusion(f32[1024,6400]{1,0:T(8,128)} %get-tuple-element.26, f32[1024]{0:T(1024)S(1)} %bitcast.70, f32[1024]{0:T(1024)S(1)} %get-tuple-element.11, s32[1024]{0:T(1024)S(1)} %bitcast.69, f32[1024]{0:T(1024)S(1)} %pmax.7), kind=kLoop, calls=%fused_computation.2 | loop fusion | flops 45875200 | bytes 39337984 | tf_op jit(solution)/shard_map/convert_element_type | solution.py:33
  176.1 35.7 %convert_convert_fusion = f32[1024,2048]{1,0:T(8,128)} fusion(bf16[1024,6400]{1,0:T(8,128)(2,1)} %fusion.1, bf16[2048,6400]{1,0:T(8,128)(2,1)} %param.17), kind=kOutput, calls=%fused_computation.19 | convolution fusion | flops 26847739904 | bytes 47710208 | tf_op jit(solution)/shard_map/dot_general | solution.py:36
  211.9 0.0 all-reduce.3.cloned.1.call-update
  211.9 0.3 reduce-scatter.2.cloned.1.call-start
  212.2 35.7 %fusion.12 = f32[2048,6400]{1,0:T(8,128)} fusion(bf16[1024,2048]{1,0:T(8,128)(2,1)} %copy-done.1, bf16[1024,6400]{1,0:T(8,128)(2,1)} %fusion.1), kind=kOutput, calls=%fused_computation.37 | convolution fusion | flops 26843545600 | bytes 69730304 | tf_op jit(solution)/shard_map/dot_general | solution.py:34
  247.9 0.0 copy-start
  247.9 0.0 copy-start.3
  247.9 0.0 copy-start.5
  247.9 0.0 reduce-scatter.2.cloned.1.call-update
  247.9 0.0 copy-start.6
  247.9 100.2 %all-reduce.3.cloned.1.call-done = f32[1024,2048]{1,0:T(8,128)} async-done(((f32[1024,2048]{1,0:T(8,128)}), f32[1024,2048]{1,0:T(8,128)}) %all-reduce.3.cloned.1.call-update) | async-done | bytes 8388624 | tf_op jit(solution)/shard_map/psum | solution.py:37
  348.1 0.0 copy-done
  348.1 0.0 copy-done.3
  348.1 0.0 copy-done.5
  348.1 4.9 fusion.5
  353.0 0.0 copy-done.6
  353.0 6.8 %multiply_convert_fusion = (bf16[2,512,2048]{2,1,0:T(8,128)(2,1)}, f32[2,2048]{1,0:T(2,128)S(1)}) fusion(f32[2,512]{1,0:T(2,128)S(1)} %div.36, f32[2,512]{1,0:T(2,128)S(1)} %copy-done.6, f32[2,2048]{1,0:T(2,128)S(1)} %copy-done.3, bf16[1,1,512,2048]{3,2,0,1:T(8,128)(2,1)S(1)} %bitcast.61, bf16[1,1,512,2048]{3,2,0,1:T(8,128)(2,1)} %bitcast.65, ...), kind=kLoop, calls=%fused_computation.17 | loop fusion | flops 20967424 | bytes 16818176 | tf_op jit(solution)/shard_map/convert_element_type | solution.py:41
  359.8 24.1 %all-reduce = (f32[]{:T(128)}, f32[2,2048]{1,0:T(2,128)S(1)}) all-reduce(f32[]{:T(128)} %get-tuple-element.10, f32[2,2048]{1,0:T(2,128)S(1)} %get-tuple-element.13), channel_id=1, replica_groups=mesh['tp'=16,'dp'=8] {'dp'}, use_global_device_ids=true, to_apply=%region_10.11 | all-reduce | flops 4097 | bytes 32776 | tf_op jit(solution)/shard_map/psum | solution.py:31
  383.9 0.6 fusion.9
  384.5 4.8 fusion.8
  389.3 113.3 %reduce-scatter.2.cloned.1.call-done = f32[256,6400]{1,0:T(8,128)} async-done(((f32[2048,6400]{1,0:T(8,128)}), f32[256,6400]{1,0:T(8,128)}) %reduce-scatter.2.cloned.1.call-update) | async-done | bytes 6553616 | tf_op jit(solution)/shard_map/reduce_scatter | solution.py:35
  (8 shorter events, 0.1 us)
Async XLA Ops:
  8.0 340.1 %all-reduce.3.cloned.1.call-start = ((), (), s32[]{:S(2)}) async-start(), calls=%async_computation.1 | async-start | bytes 16777216 | tf_op jit(solution)/shard_map/psum | solution.py:37
  11.3 0.8 copy-start.4
  12.1 0.6 copy-start.2
  15.4 35.2 %copy-start.1 = (bf16[1024,2048]{1,0:T(8,128)(2,1)}, bf16[1024,2048]{1,0:T(8,128)(2,1)S(1)}, u32[]{:S(2)}) copy-start(bf16[1024,2048]{1,0:T(8,128)(2,1)S(1)} %fusion.3) | copy-start | bytes 12582916
  15.4 70.7 %copy-start.9 = (s32[1,512]{1,0:T(1,128)S(1)}, s32[1,512]{1,0:T(1,128)}, u32[]{:S(2)}) copy-start(s32[1,512]{1,0:T(1,128)} %param.12) | copy-start | bytes 6148
  15.4 70.7 %copy-start.10 = (s32[1,512]{1,0:T(1,128)S(1)}, s32[1,512]{1,0:T(1,128)}, u32[]{:S(2)}) copy-start(s32[1,512]{1,0:T(1,128)} %param.11) | copy-start | bytes 6148
  86.2 39.5 %copy-start.8 = (f32[1,512]{1,0:T(1,128)S(1)}, f32[1,512]{1,0:T(1,128)}, u32[]{:S(2)}) copy-start(f32[1,512]{1,0:T(1,128)} %param.13) | copy-start | bytes 6148
  86.2 40.1 %copy-start.7 = (f32[1,512]{1,0:T(1,128)S(1)}, f32[1,512]{1,0:T(1,128)}, u32[]{:S(2)}) copy-start(f32[1,512]{1,0:T(1,128)} %param.14) | copy-start | bytes 6148
  211.9 290.7 %reduce-scatter.2.cloned.1.call-start = ((), (), s32[]{:S(2)}) async-start(), calls=%async_computation.2 | async-start | bytes 58982400 | tf_op jit(solution)/shard_map/reduce_scatter | solution.py:35
  247.9 100.2 %copy-start = (bf16[1,512,2048]{2,1,0:T(8,128)(2,1)S(1)}, bf16[1,512,2048]{2,1,0:T(8,128)(2,1)}, u32[]{:S(2)}) copy-start(bf16[1,512,2048]{2,1,0:T(8,128)(2,1)} %param.10) | copy-start | bytes 6291460
  247.9 100.2 %copy-start.3 = (f32[2,2048]{1,0:T(2,128)S(1)}, f32[2,2048]{1,0:T(2,128)}, u32[]{:S(2)}) copy-start(f32[2,2048]{1,0:T(2,128)} %copy-done.2) | copy-start | bytes 49156
  247.9 100.2 %copy-start.5 = (f32[1,4,2,128]{3,1,2,0:T(4,128)S(1)}, f32[1,4,2,128]{3,1,2,0:T(4,128)}, u32[]{:S(2)}) copy-start(f32[1,4,2,128]{3,1,2,0:T(4,128)} %copy-done.4) | copy-start | bytes 12292
  247.9 105.1 %copy-start.6 = (f32[2,512]{1,0:T(2,128)S(1)}, f32[2,512]{1,0:T(2,128)}, u32[]{:S(2)}) copy-start(f32[2,512]{1,0:T(2,128)} %get-tuple-element.21) | copy-start | bytes 12292
Sparse Core Ops, SparseCore 0:
  212.0 136.0 all-reduce.2
Sparse Core Ops, SparseCore 1:
  248.0 254.5 reduce-scatter.1
where the time goes:
time: 510 us
  waiting for transfers between devices  213 us (42%)
  blocking collectives  115 us (23%)
  matrix products  107 us (21%)
  other arithmetic  50.4 us (10%)
  between operations  17 us (3%)
  local copies, waits for them, and re-layouts  6.75 us (1%)
    reduce_scatter x1, waiting for transfers between devices, local_step(): grad_w = lax.psum_scatter(grad_w, 'dp', scatter_dimension=0, tiled=True)  113 us
    psum x1, waiting for transfers between devices, local_step(): lax.psum(grad_part.astype(jnp.float32), 'tp').reshape(2, rows, d_model)  100 us
    dot_general x1, matrix products, local_step(): lax.dot_general(grad_z, w_out, (((1,), (1,)), ((), ())), preferred_elemen...  35.7 us
    dot_general x1, matrix products, local_step(): lax.dot_general(u_rows, grad_z, (((0,), (0,)), ((), ())), preferred_eleme...  35.7 us
    pmax x1, blocking collectives, local_step(): row_max = lax.pmax(jnp.max(logits, axis=-1), 'tp')  35.5 us
    dot_general x1, matrix products, local_step(): logits = jnp.dot(u_rows, w_out, preferred_element_type=jnp.float32)  35.2 us
    psum x1, blocking collectives, local_step(): lax.psum(jnp.stack([jnp.sum(shifted, axis=-1), jnp.sum(jnp.where(is_targe...  29 us
    psum x1, blocking collectives, local_step(): lax.psum(jnp.stack([jnp.sum(weight_main), jnp.sum(weight_mtp)]), 'dp')  26.8 us
  transfers between devices with their start and end apart: 2, of which 2 were waited for; matrix products, arithmetic and copies ran while one was open for 10% of the time, Pallas kernels for 0%

commit v1 on v0

v1 whole, which is shorter than its diff:
```python
import functools

import jax
import jax.numpy as jnp
from jax import lax
from jax.experimental import pallas as pl
from jax.experimental.pallas import tpu as pltpu
from jax.sharding import PartitionSpec as P

NORM_EPS = 1e-6
MTP_LAMBDA = 0.3
MESH = pl.DeviceIdType.MESH
F32 = jnp.float32
BF16 = jnp.bfloat16
ANY = pl.BlockSpec(memory_space=pl.ANY)
VMEM = pl.BlockSpec(memory_space=pltpu.VMEM)


def columns(row, width=128):
    return jnp.broadcast_to(row, (width, row.shape[1])).T


def logits_kernel(n_tp, n_dp, chunk, hm, ht, gain, lab_m, lab_t, wt_m, wt_t, w, z, u_out, st, lpart, h_v, u_v, w_v, z_v, m_v, s_v, t_v,
                  lab_v, send_v, land, wsend, wland, psend, pland, sem_h, sem_u, sem_w, sem_z, ssem, rsem, wssem, wrsem, pssem, prsem):
    seq, depth = hm.shape
    rows, vocab = z.shape
    steps = vocab // chunk
    tp, dp = lax.axis_index("tp"), lax.axis_index("dp")
    partner = lax.rem(dp // 2 + 1, 2) * 2 + (dp // 4) * 4 + lax.rem(dp, 2)

    loads = [pltpu.make_async_copy(src, h_v.at[pl.ds(i * seq, seq), :], sem_h.at[i]) for i, src in enumerate((hm, ht))]

    def w_copy(i, slot):
        return pltpu.make_async_copy(w.at[:, pl.ds(pl.multiple_of(i * chunk, 128), chunk)], w_v.at[slot], sem_w.at[slot])

    def z_copy(i, slot):
        return pltpu.make_async_copy(z_v.at[slot], z.at[:, pl.ds(pl.multiple_of(i * chunk, 128), chunk)], sem_z.at[slot])

    for c in loads:
        c.start()
    w_copy(0, 0).start()
    barrier = pltpu.get_barrier_semaphore()
    for d in range(1, n_tp):
        pl.semaphore_signal(barrier, inc=1, device_id={"tp": lax.rem(tp + d, n_tp), "dp": dp}, device_id_type=MESH)
    for d in range(1, n_dp):
        pl.semaphore_signal(barrier, inc=1, device_id={"tp": tp, "dp": lax.rem(dp + d, n_dp)}, device_id_type=MESH)

    m_v[...] = jnp.full_like(m_v, -jnp.inf)
    s_v[...] = jnp.zeros_like(s_v)
    t_v[...] = jnp.zeros_like(t_v)
    first = (tp * vocab).astype(F32)
    lab_v[pl.ds(0, seq), :] = columns(lab_m[...].astype(F32) - first)
    lab_v[pl.ds(seq, seq), :] = columns(lab_t[...].astype(F32) - first)
    wrow = lax.broadcasted_iota(jnp.int32, (8, 128), 0)
    wsend[...] = jnp.where(wrow == 0, jnp.sum(wt_m[...]), jnp.sum(wt_t[...]))
    wland[dp] = wsend[...]

    for c in loads:
        c.wait()
    for half in range(2):
        g = gain[pl.ds(half, 1), :]

        @pl.loop(0, seq // 128)
        def _(i):
            r = pl.ds(pl.multiple_of(half * seq + i * 128, 128), 128)
            x = h_v[r, :].astype(F32)
            inv = lax.rsqrt(jnp.mean(x * x, axis=-1, keepdims=True) + NORM_EPS)
            u_v[r, :] = (x * inv * g).astype(BF16)

    u_copy = pltpu.make_async_copy(u_v, u_out, sem_u)
    u_copy.start()
    lane = lax.broadcasted_iota(jnp.int32, (rows, 128), 1).astype(F32)

    @pl.loop(0, steps)
    def _(i):
        slot = lax.rem(i, 2)
        w_copy(i, slot).wait()

        @pl.when(i + 1 < steps)
        def _():
            w_copy(i + 1, 1 - slot).start()

        @pl.when(i >= 2)
        def _():
            z_copy(i - 2, slot).wait()

        m, s, t = m_v[...], s_v[...], t_v[...]
        rel = lab_v[...] - (i * chunk).astype(F32)
        for n in range(chunk // 256):
            cols = slice(n * 256, (n + 1) * 256)
            zz = jnp.dot(u_v[...], w_v[slot, :, cols], preferred_element_type=F32)
            z_v[slot, :, cols] = zz
            za, zb = zz[:, :128], zz[:, 128:]
            new = jnp.maximum(m, jnp.maximum(za, zb))
            s = s * jnp.exp(m - new) + (jnp.exp(za - new) + jnp.exp(zb - new))
            t = jnp.where(rel == lane + n * 256, za, t)
            t = jnp.where(rel == lane + (n * 256 + 128), zb, t)
            m = new
        m_v[...], s_v[...], t_v[...] = m, s, t
        z_copy(i, slot).start()

    pl.semaphore_wait(barrier, n_tp + n_dp - 2)
    wcopies = []
    for d in range(1, n_dp):
        peer = lax.rem(dp + d, n_dp)
        c = pltpu.make_async_remote_copy(wsend, wland.at[dp], wssem.at[d], wrsem.at[dp], device_id={"tp": tp, "dp": peer}, device_id_type=MESH)
        c.start()
        wcopies.append(c)
    mt = m_v[...].T
    top = jnp.max(mt, axis=0, keepdims=True)
    total = jnp.sum(s_v[...].T * jnp.exp(mt - top), axis=0, keepdims=True)
    hit = jnp.sum(t_v[...].T, axis=0, keepdims=True)
    srow = lax.broadcasted_iota(jnp.int32, (8, rows), 0)
    mine = jnp.where(srow == 0, top + jnp.log(total), hit)
    send_v[...] = mine
    land[tp] = mine
    copies = []
    for d in range(1, n_tp):
        peer = lax.rem(tp + d, n_tp)
        c = pltpu.make_async_remote_copy(send_v, land.at[tp], ssem.at[d], rsem.at[tp], device_id={"tp": peer, "dp": dp}, device_id_type=MESH)
        c.start()
        copies.append(c)
    for d in range(1, n_dp):
        src = lax.rem(dp + d, n_dp)
        pltpu.make_async_copy(wland.at[src], wland.at[src], wrsem.at[src]).wait()
    sums = wland[0]
    for d in range(1, n_dp):
        sums = sums + wland[d]
    coef_m = 1.0 / sums[0:1, 0:1]
    coef_t = MTP_LAMBDA / sums[1:2, 0:1]
    rw = jnp.concatenate([wt_m[...] * coef_m, wt_t[...] * coef_t], axis=1)
    lab = jnp.concatenate([lab_m[...], lab_t[...]], axis=1).astype(F32)
    for d in range(1, n_tp):
        src = lax.rem(tp + d, n_tp)
        pltpu.make_async_copy(land.at[src], land.at[src], rsem.at[src]).wait()
    top = land[0]
    for d in range(1, n_tp):
        top = jnp.maximum(top, land[d])
    acc = jnp.zeros_like(top)
    hits = jnp.zeros_like(top)
    for d in range(n_tp):
        acc = acc + jnp.exp(land[d] - top)
        hits = hits + land[d]
    lse = (top + jnp.log(acc))[0:1, :]
    hit = hits[1:2, :]
    lpart[...] = jnp.broadcast_to(jnp.sum(rw * (lse - hit)), (8, 128))
    mine = jnp.where(srow == 0, lse, jnp.where(srow == 1, rw, lab - first))
    psend[...] = mine
    st[0] = mine
    c = pltpu.make_async_remote_copy(psend, pland, pssem, prsem, device_id={"tp": tp, "dp": partner}, device_id_type=MESH)
    c.start()
    c.wait()
    st[1] = pland[...]
    for c in wcopies + copies:
        c.wait_send()
    z_copy(steps - 2, (steps - 2) % 2).wait()
    z_copy(steps - 1, (steps - 1) % 2).wait()
    u_copy.wait()


def logits(n_tp, n_dp, hm, ht, gain, lab_m, lab_t, wt_m, wt_t, w):
    seq, depth = hm.shape
    rows, vocab = 2 * seq, w.shape[1]
    chunk = 1280
    dma = pltpu.SemaphoreType.DMA
    return pl.pallas_call(
        functools.partial(logits_kernel, n_tp, n_dp, chunk),
        out_shape=(
            jax.ShapeDtypeStruct((rows, vocab), F32),
            jax.ShapeDtypeStruct((rows, depth), BF16),
            jax.ShapeDtypeStruct((2, 8, rows), F32),
            jax.ShapeDtypeStruct((8, 128), F32),
        ),
        in_specs=[ANY, ANY, VMEM, VMEM, VMEM, VMEM, VMEM, ANY],
        out_specs=(ANY, ANY, VMEM, VMEM),
        scratch_shapes=[
            pltpu.VMEM((rows, depth), BF16),
            pltpu.VMEM((rows, depth), BF16),
            pltpu.VMEM((2, depth, chunk), BF16),
            pltpu.VMEM((2, rows, chunk), F32),
            pltpu.VMEM((rows, 128), F32),
            pltpu.VMEM((rows, 128), F32),
            pltpu.VMEM((rows, 128), F32),
            pltpu.VMEM((rows, 128), F32),
            pltpu.VMEM((8, rows), F32),
            pltpu.VMEM((n_tp, 8, rows), F32),
            pltpu.VMEM((8, 128), F32),
            pltpu.VMEM((n_dp, 8, 128), F32),
            pltpu.VMEM((8, rows), F32),
            pltpu.VMEM((8, rows), F32),
            dma((2,)), dma, dma((2,)), dma((2,)),
            dma((n_tp,)), dma((n_tp,)), dma((n_dp,)), dma((n_dp,)), dma, dma,
        ],
        compiler_params=pltpu.CompilerParams(vmem_limit_bytes=62 * 2**20, collective_id=0, has_side_effects=True),
        cost_estimate=pl.CostEstimate(flops=2 * rows * depth * vocab, bytes_accessed=2 * depth * vocab, transcendentals=0),
        name="logits",
    )(hm, ht, gain, lab_m, lab_t, wt_m, wt_t, w)


def grad_logits(z, lse, rw, lab, col):
    lane = lax.broadcasted_iota(jnp.int32, z.shape, 1).astype(F32)
    p = jnp.exp(z - lse)
    return rw * jnp.where(lab - col == lane, p - 1.0, p)


def du_kernel(chunk, z, w, st, du, z_v, w_v, e_v, acc, lse_v, rw_v, lab_v, sem_z, sem_w, sem_o):
    rows, vocab = z.shape
    steps = vocab // chunk

    def w_copy(i, slot):
        return pltpu.make_async_copy(w.at[:, pl.ds(pl.multiple_of(i * chunk, 128), chunk)], w_v.at[slot], sem_w.at[slot])

    def z_copy(i, slot):
        return pltpu.make_async_copy(z.at[:, pl.ds(pl.multiple_of(i * chunk, 128), chunk)], z_v.at[slot], sem_z.at[slot])

    z_copy(0, 0).start()
    w_copy(0, 0).start()
    lse_v[...] = columns(st[0, 0:1, :])
    rw_v[...] = columns(st[0, 1:2, :])
    lab_v[...] = columns(st[0, 2:3, :])
    acc[...] = jnp.zeros_like(acc)

    @pl.loop(0, steps)
    def _(i):
        slot = lax.rem(i, 2)
        z_copy(i, slot).wait()
        w_copy(i, slot).wait()

        @pl.when(i + 1 < steps)
        def _():
            z_copy(i + 1, 1 - slot).start()
            w_copy(i + 1, 1 - slot).start()

        col = (i * chunk).astype(F32)
        for g in range(chunk // 128):
            cols = slice(g * 128, (g + 1) * 128)
            e_v[:, cols] = grad_logits(z_v[slot, :, cols], lse_v[...], rw_v[...], lab_v[...], col + g * 128).astype(BF16)
        for n in range(acc.shape[1] // 512):
            cols = slice(n * 512, (n + 1) * 512)
            acc[:, cols] += lax.dot_general(e_v[...], w_v[slot, cols, :], (((1,), (1,)), ((), ())), preferred_element_type=F32)

    acc[...] = acc[...].astype(BF16).astype(F32)
    c = pltpu.make_async_copy(acc, du, sem_o)
    c.start()
    c.wait()


def du_partial(z, w, st):
    rows, vocab = z.shape
    depth = w.shape[0]
    chunk = 640
    dma = pltpu.SemaphoreType.DMA
    return pl.pallas_call(
        functools.partial(du_kernel, chunk),
        out_shape=jax.ShapeDtypeStruct((rows, depth), F32),
        in_specs=[ANY, ANY, VMEM],
        out_specs=ANY,
        scratch_shapes=[
            pltpu.VMEM((2, rows, chunk), F32),
            pltpu.VMEM((2, depth, chunk), BF16),
            pltpu.VMEM((rows, chunk), BF16),
            pltpu.VMEM((rows, depth), F32),
            pltpu.VMEM((rows, 128), F32),
            pltpu.VMEM((rows, 128), F32),
            pltpu.VMEM((rows, 128), F32),
            dma((2,)), dma((2,)), dma,
        ],
        compiler_params=pltpu.CompilerParams(vmem_limit_bytes=62 * 2**20),
        cost_estimate=pl.CostEstimate(flops=2 * rows * depth * vocab, bytes_accessed=2 * depth * vocab, transcendentals=0),
        name="du_partial",
    )(z, w, st)


def head_kernel(first, wide, u_own, u_par, z, w, st, after, out, u_v, up_v, w_v, z_v, et_v, g_v, own_v, sum_v, one_v, o_v,
                lse_v, rw_v, lab_v, sem_u, sem_p, sem_w, sem_z, sem_o, d_send, d_recv, b_send, b_recv, f_send, f_recv):
    del after
    rows, depth = u_own.shape
    half = z.shape[1] // 2
    tp, dp = lax.axis_index("tp"), lax.axis_index("dp")
    x, core = dp // 2, lax.rem(dp, 2)
    side = lax.rem((x + 1) // 2, 2)
    mate, far = x + 1 - 2 * lax.rem(x, 2), 3 - x
    far_mate = far + 1 - 2 * lax.rem(far, 2)

    def at(chip, c):
        return {"tp": tp, "dp": 2 * chip + c}

    barrier = pltpu.get_barrier_semaphore()
    for peer in (at(x, 1 - core), at(far, core), at(mate, core)):
        pl.semaphore_signal(barrier, inc=1, device_id=peer, device_id_type=MESH)

    blocks = [2 * j + 1 - core for j in range(4)] + [2 * j + core for j in range(4)]

    def u_copy(i):
        return pltpu.make_async_copy(u_own.at[:, pl.ds(pl.multiple_of(blocks[i] * 256, 256), 256)],
                                     u_v.at[pl.ds(0, rows), pl.ds(i * 256, 256)], sem_u.at[i])

    def p_copy(i, slot):
        return pltpu.make_async_copy(u_par.at[:, pl.ds(pl.multiple_of(blocks[i] * 256, 256), 256)], up_v.at[slot], sem_p.at[slot])

    def w_copies(c0, width, slot):
        cols = pl.ds(pl.multiple_of(side * half + c0, 128), width)
        return [pltpu.make_async_copy(w.at[pl.ds(pl.multiple_of(blocks[i] * 256, 256), 256), cols],
                                      w_v.at[slot, pl.ds(i * 256, 256), pl.ds(0, width)], sem_w.at[slot, i]) for i in range(8)]

    def z_copy(c0, width, slot):
        cols = pl.ds(pl.multiple_of(side * half + c0, 128), width)
        return pltpu.make_async_copy(z.at[:, cols], z_v.at[slot, :, pl.ds(0, width)], sem_z.at[slot])

    def fetch(c0, width, slot):
        for c in w_copies(c0, width, slot) + [z_copy(c0, width, slot)]:
            c.start()

    fetch(0, first, 0)
    for i in range(8):
        u_copy(i).start()
    p_copy(0, 0).start()
    p_copy(1, 1).start()
    for k in range(2):
        r = pl.ds(k * rows, rows)
        lse_v[r, :] = columns(st[k, 0:1, :])
        rw_v[r, :] = columns(st[k, 1:2, :])
        lab_v[r, :] = columns(st[k, 2:3, :])
    for i in range(8):
        p_copy(i, i % 2).wait()
        u_v[pl.ds(rows, rows), pl.ds(i * 256, 256)] = up_v[i % 2].astype(BF16)
        if i + 2 < 8:
            p_copy(i + 2, i % 2).start()
    for i in range(8):
        u_copy(i).wait()

    def d_copy(k, c0, width, slot):
        return pltpu.make_async_remote_copy(g_v.at[slot, pl.ds(0, width), :], sum_v.at[pl.ds(c0, width), :], d_send.at[slot], d_recv.at[k],
                                            device_id=at(x, 1 - core), device_id_type=MESH)

    def b_copy(k, c0, width, which):
        chip = (far_mate, far)[which]
        return pltpu.make_async_remote_copy(sum_v.at[pl.ds(c0, width), pl.ds(pl.multiple_of(chip * 256, 256), 256)],
                                            one_v.at[which, pl.ds(c0, width), :], b_send.at[2 * k + which], b_recv.at[2 * k + which],
                                            device_id=at(far, core), device_id_type=MESH)

    def f_copy(k, c0, width, slot):
        return pltpu.make_async_remote_copy(o_v.at[0, slot, :, pl.ds(0, width)], out.at[:, pl.ds(pl.multiple_of(side * half + c0, 128), width)],
                                            f_send.at[slot], f_recv.at[k], device_id=at(mate, core), device_id_type=MESH)

    def f_arrival(k, c0, width):
        dst = out.at[:, pl.ds(pl.multiple_of((1 - side) * half + c0, 128), width)]
        return pltpu.make_async_copy(dst, dst, f_recv.at[k])

    def o_copy(c0, width, slot):
        return pltpu.make_async_copy(o_v.at[1, slot, :, pl.ds(0, width)], out.at[:, pl.ds(pl.multiple_of(side * half + c0, 128), width)], sem_o.at[slot])

    def make(k, c0, width, slot):
        for c in w_copies(c0, width, slot) + [z_copy(c0, width, slot)]:
            c.wait()
        col = (side * half + c0).astype(F32)
        own, par = pl.ds(0, rows), pl.ds(rows, rows)
        for g in range(width // 128):
            cols = slice(g * 128, (g + 1) * 128)
            e = grad_logits(z_v[slot, :, cols], lse_v[own, :], rw_v[own, :], lab_v[own, :], col + g * 128)
            et_v[cols, own] = e.T.astype(BF16)
        step = min(width, 256)
        for n in range(width // step):
            zz = jnp.dot(u_v[par, :], w_v[slot, :, n * step:(n + 1) * step], preferred_element_type=F32)
            for g in range(step // 128):
                c1 = n * step + g * 128
                e = grad_logits(zz[:, g * 128:(g + 1) * 128], lse_v[par, :], rw_v[par, :], lab_v[par, :], col + c1)
                et_v[c1:c1 + 128, par] = e.T.astype(BF16)
        et = et_v[pl.ds(0, width), :]
        g_v[slot, pl.ds(0, width), :] = jnp.dot(et, u_v[:, :1024], preferred_element_type=F32)
        d_copy(k, c0, width, slot).start()
        own_v[pl.ds(0, width), :] = jnp.dot(et, u_v[:, 1024:], preferred_element_type=F32)

    def add(k, c0, width, slot):
        d_copy(k, c0, width, slot).wait_recv()
        r = pl.ds(c0, width)
        sum_v[r, :] += own_v[pl.ds(0, width), :]
        for which in range(2):
            b_copy(k, c0, width, which).start()

    def close(k, c0, width, slot, free):
        @pl.when(free)
        def _():
            f_copy(k, c0, wide, slot).wait_send()
            o_copy(c0, wide, slot).wait()
        r = pl.ds(c0, width)
        for which, chip in enumerate((mate, x)):
            b_copy(k, c0, width, which).wait_recv()
            total = sum_v[r, pl.ds(pl.multiple_of(chip * 256, 256), 256)] + one_v[which, r, :]
            o_v[which, slot, :, pl.ds(0, width)] = total.T
            (f_copy if which == 0 else lambda k, *a: o_copy(*a))(k, c0, width, slot).start()

    n = (half - first) // wide
    start = lambda k: pl.multiple_of(first + (k - 1) * wide, 128)
    fetch(start(1), wide, 1)
    pl.semaphore_wait(barrier, 3)
    make(0, 0, first, 0)
    add(0, 0, first, 0)

    @pl.loop(1, n + 1)
    def _(k):
        slot = lax.rem(k, 2)

        @pl.when(k < n)
        def _():
            fetch(start(k + 1), wide, 1 - slot)

        @pl.when(k == 2)
        def _():
            d_copy(0, 0, first, 0).wait_send()

        @pl.when(k > 2)
        def _():
            d_copy(k - 2, start(k - 2), wide, slot).wait_send()

        make(k, start(k), wide, slot)
        add(k, start(k), wide, slot)

        @pl.when(k == 1)
        def _():
            close(0, 0, first, 0, False)

        @pl.when(k == 2)
        def _():
            close(1, start(1), wide, 1, False)

        @pl.when(k == 3)
        def _():
            f_copy(0, 0, first, 0).wait_send()
            o_copy(0, first, 0).wait()
            close(2, start(2), wide, 0, False)

        @pl.when(k > 3)
        def _():
            close(k - 1, start(k - 1), wide, 1 - slot, True)

    close(n, start(n), wide, n % 2, True)
    for k in (n - 1, n):
        f_copy(k, start(k), wide, k % 2).wait_send()
        o_copy(start(k), wide, k % 2).wait()
        d_copy(k, start(k), wide, k % 2).wait_send()
    for k in range(n + 1):
        c0, width = (0, first) if k == 0 else (first + (k - 1) * wide, wide)
        f_arrival(k, c0, width).wait()
        for which in range(2):
            b_copy(k, c0, width, which).wait_send()


def head_grad(u_own, u_par, z, w, st, after):
    rows, depth = u_own.shape
    vocab = z.shape[1]
    first, wide = 128, 512
    half = vocab // 2
    n = (half - first) // wide + 1
    dma = pltpu.SemaphoreType.DMA
    return pl.pallas_call(
        functools.partial(head_kernel, first, wide),
        out_shape=jax.ShapeDtypeStruct((256, vocab), F32),
        in_specs=[ANY, ANY, ANY, ANY, VMEM, ANY],
        out_specs=ANY,
        scratch_shapes=[
            pltpu.VMEM((2 * rows, depth), BF16),
            pltpu.VMEM((2, rows, 256), F32),
            pltpu.VMEM((2, depth, wide), BF16),
            pltpu.VMEM((2, rows, wide), F32),
            pltpu.VMEM((wide, 2 * rows), BF16),
            pltpu.VMEM((2, wide, 1024), F32),
            pltpu.VMEM((wide, 1024), F32),
            pltpu.VMEM((half, 1024), F32),
            pltpu.VMEM((2, half, 256), F32),
            pltpu.VMEM((2, 2, 256, wide), F32),
            pltpu.VMEM((2 * rows, 128), F32),
            pltpu.VMEM((2 * rows, 128), F32),
            pltpu.VMEM((2 * rows, 128), F32),
            dma((8,)), dma((2,)), dma((2, 8)), dma((2,)), dma((2,)),
            dma((2,)), dma((n,)), dma((2 * n,)), dma((2 * n,)), dma((2,)), dma((n,)),
        ],
        compiler_params=pltpu.CompilerParams(vmem_limit_bytes=63 * 2**20, collective_id=1, has_side_effects=True),
        cost_estimate=pl.CostEstimate(flops=300 * 10**9, bytes_accessed=2 * depth * vocab, transcendentals=0),
        name="head_grad",
    )(u_own, u_par, z, w, st, after)


def total_kernel(n_dp, part, out, land, ssem, rsem):
    tp, dp = lax.axis_index("tp"), lax.axis_index("dp")
    barrier = pltpu.get_barrier_semaphore()
    for d in range(1, n_dp):
        pl.semaphore_signal(barrier, inc=1, device_id={"tp": tp, "dp": lax.rem(dp + d, n_dp)}, device_id_type=MESH)
    land[dp] = part[...]
    pl.semaphore_wait(barrier, n_dp - 1)
    copies = []
    for d in range(1, n_dp):
        c = pltpu.make_async_remote_copy(part, land.at[dp], ssem.at[d], rsem.at[dp],
                                         device_id={"tp": tp, "dp": lax.rem(dp + d, n_dp)}, device_id_type=MESH)
        c.start()
        copies.append(c)
    for d in range(1, n_dp):
        src = lax.rem(dp + d, n_dp)
        pltpu.make_async_copy(land.at[src], land.at[src], rsem.at[src]).wait()
    total = land[0]
    for d in range(1, n_dp):
        total = total + land[d]
    out[...] = total
    for c in copies:
        c.wait_send()


def dp_total(n_dp, part):
    dma = pltpu.SemaphoreType.DMA
    return pl.pallas_call(
        functools.partial(total_kernel, n_dp),
        out_shape=jax.ShapeDtypeStruct(part.shape, F32),
        in_specs=[VMEM],
        out_specs=VMEM,
        scratch_shapes=[pltpu.VMEM((n_dp,) + part.shape, F32), dma((n_dp,)), dma((n_dp,))],
        compiler_params=pltpu.CompilerParams(collective_id=2, has_side_effects=True),
        name="dp_total",
    )(part)


def solution(mesh):
    n_tp, n_dp = mesh.shape["tp"], mesh.shape["dp"]

    def local_step(h_main, h_mtp, labels_main, labels_mtp, weight_main, weight_mtp, gain_final, gain_mtp, w_out):
        batch_loc, seq_len, depth = h_main.shape
        rows = 2 * seq_len
        share = rows // n_tp
        tp = lax.axis_index("tp")
        hm, ht = h_main[0], h_mtp[0]
        gain = jnp.stack([gain_final, gain_mtp])
        per = seq_len // share
        at = lax.rem(tp, per) * share
        is_main = tp < per
        x = jnp.where(is_main, lax.dynamic_slice_in_dim(hm, at, share), lax.dynamic_slice_in_dim(ht, at, share)).astype(F32)
        g = jnp.where(is_main, gain_final, gain_mtp)[None, :]
        inv = lax.rsqrt(jnp.mean(x * x, axis=-1, keepdims=True) + NORM_EPS)
        normed = x * inv
        u_share = lax.optimization_barrier((normed * g).astype(BF16)).astype(F32)
        swap = [(d, (d // 2 ^ 1) * 2 + d % 2) for d in range(n_dp)]
        u_par = lax.all_gather(lax.ppermute(u_share, "dp", swap), "tp", axis=0, tiled=True)

        z, u_own, st, lpart = logits(n_tp, n_dp, hm, ht, gain, labels_main, labels_mtp, weight_main, weight_mtp, w_out)
        du = du_partial(z, w_out, st)
        grad_w = head_grad(u_own, u_par, z, w_out, st, du)
        gu = lax.psum_scatter(du, "tp", scatter_dimension=0, tiled=True)
        gn = gu * g
        gx = inv * (gn - normed * jnp.mean(gn * normed, axis=-1, keepdims=True))
        gg = jnp.sum(gu * normed, axis=0, keepdims=True)
        gg = jnp.concatenate([jnp.where(is_main, gg, 0.0), jnp.where(is_main, 0.0, gg), jnp.zeros((6, depth), F32)])
        pack = lax.optimization_barrier(jnp.concatenate([gx.astype(BF16).astype(F32), gg]))
        pack = lax.optimization_barrier(lax.all_gather(pack, "tp", axis=0, tiled=False))
        grad_h = pack[:, :share].astype(BF16).reshape(2, batch_loc, seq_len, depth)
        gains = jnp.sum(pack[:, share:], axis=0)
        row = lax.broadcasted_iota(jnp.int32, (8, depth), 0)
        total = dp_total(n_dp, jnp.where(row == 2, lpart[0, 0], gains))
        return total[2, 0], grad_h[0], grad_h[1], grad_w, total[0], total[1]

    row_spec = P("dp", None)
    return jax.shard_map(
        local_step,
        mesh=mesh,
        in_specs=(P("dp", None, None), P("dp", None, None), row_spec, row_spec, row_spec, row_spec, P(None), P(None), P(None, "tp")),
        out_specs=(P(), P("dp", None, None), P("dp", None, None), P("dp", "tp"), P(None), P(None)),
        check_vma=False,
    )
```

time: 510 us -> 481 us (0.943)
  Pallas kernels: 0 us -> 272 us
  blocking collectives: 115 us -> 0 us
  matrix products: 107 us -> 0 us
  waiting for transfers between devices: 213 us -> 161 us
  other arithmetic: 50.4 us -> 15.9 us
  local copies, waits for them, and re-layouts: 6.75 us -> 15.7 us
    pallas_call x0 -> x4, Pallas kernels: none -> 272 us  [the longest x1 162 us: head_grad(): pl.pallas_call(functools.partial(head_kernel, first, wide), out_shape=jax...]
    dot_general x3 -> x0, matrix products: 107 us -> none  [the longest x1 35.7 us: local_step(): lax.dot_general(grad_z, w_out, (((1,), (1,)), ((), ())), preferred_elemen...]
    psum x1 -> x0, waiting for transfers between devices: 100 us -> none  [local_step(): lax.psum(grad_part.astype(jnp.float32), 'tp').reshape(2, rows, d_model)]
    psum x3 -> x0, blocking collectives: 79.9 us -> none  [the longest x1 29 us: local_step(): lax.psum(jnp.stack([jnp.sum(shifted, axis=-1), jnp.sum(jnp.where(is_targe...]
    all_gather x0 -> x2, waiting for transfers between devices: none -> 68.2 us  [the longest x1 68.2 us: local_step(): lax.all_gather(lax.ppermute(u_share, 'dp', swap), 'tp', axis=0, tiled=True)]
    pmax x1 -> x0, blocking collectives: 35.5 us -> none  [local_step(): row_max = lax.pmax(jnp.max(logits, axis=-1), 'tp')]
    reduce_scatter x1, waiting for transfers between devices: 113 us -> 83 us  [local_step(): gu = lax.psum_scatter(du, 'tp', scatter_dimension=0, tiled=True)]
    convert_element_type x3 -> x2, other arithmetic: 27.9 us -> 1.24 us  [the longest x1 1.2 us: local_step(): gx.astype(BF16).astype(F32)]
  transfers between devices with their start and end apart: 2 -> 4, of which waited for: 2 -> 3; matrix products, arithmetic and copies ran while one was open for 10% -> 1% of each run, Pallas kernels for 0% -> 34%
where the time goes in v1:
time: 481 us; the launch traced here: 480 us
  Pallas kernels  272 us (57%)
  waiting for transfers between devices  161 us (33%)
  other arithmetic  15.9 us (3%)
  local copies, waits for them, and re-layouts  15.7 us (3%)
  between operations  13.9 us (3%)
    pallas_call x1, Pallas kernels, head_grad(): pl.pallas_call(functools.partial(head_kernel, first, wide), out_shape=jax...  162 us
    reduce_scatter x1, waiting for transfers between devices, local_step(): gu = lax.psum_scatter(du, 'tp', scatter_dimension=0, tiled=True)  83 us
    all_gather x1, waiting for transfers between devices, local_step(): lax.all_gather(lax.ppermute(u_share, 'dp', swap), 'tp', axis=0, tiled=True)  68.2 us
    pallas_call x1, Pallas kernels, logits(): pl.pallas_call(functools.partial(logits_kernel, n_tp, n_dp, chunk), out_s...  52.4 us
    pallas_call x1, Pallas kernels, du_partial(): pl.pallas_call(functools.partial(du_kernel, chunk), out_shape=jax.ShapeDt...  43.9 us
    pallas_call x1, Pallas kernels, dp_total(): pl.pallas_call(functools.partial(total_kernel, n_dp), out_shape=jax.Shape...  12.8 us
    ppermute x1, waiting for transfers between devices, local_step(): lax.ppermute(u_share, 'dp', swap)  9.93 us
  transfers between devices with their start and end apart: 4, of which 3 were waited for; matrix products, arithmetic and copies ran while one was open for 1% of the time, Pallas kernels for 34%

profile of v1, /device:TPU:1, one launch (start us, length us, event | category | flops | bytes accessed | tf_op | source)
XLA Modules:
  0.0 479.8 jit_solution(10260036787753791710)
XLA Ops:
  7.2 0.0 reduce-scatter.2.cloned.1.call-start
  7.2 1.3 pad_maximum_fusion.gain
  8.6 52.4 %logits.1 = (f32[1024,6400]{1,0:T(8,128)}, bf16[1024,2048]{1,0:T(8,128)(2,1)}, f32[2,8,1024]{2,1,0:T(8,128)}, f32[8,128]{1,0:T(8,128)}) custom-call(bf16[512,2048]{1,0:T(8,128)(2,1)} %bitcast.26, bf16[512,2048]{1,0:T(8,128)(2,1)} %bitcast.27, f32[2,2048]{1,0:T(2,128)} %pad_maximum_fusion.gain, s32[1,512]{1,0:T(1,128)} %lab_m.1, s32[1,512]{1,0:T(1,128)} %lab_t.1, ...), custom_call_target="tpu_custom_call" | custom-call | flops 26843545600 | bytes 26214400 | tf_op jit(solution)/shard_map/logits/pallas_call | solution.py:166
  61.0 43.9 %du_partial.1.after = f32[1024,2048]{1,0:T(8,128)} custom-call(f32[1024,6400]{1,0:T(8,128)} %get-tuple-element.11.z, bf16[2048,6400]{1,0:T(8,128)(2,1)} %w.5, f32[2,8,1024]{2,1,0:T(8,128)} %get-tuple-element.12.st), custom_call_target="tpu_custom_call" | custom-call | flops 26843545600 | bytes 26214400 | tf_op jit(solution)/shard_map/du_partial/pallas_call | solution.py:253
  104.9 0.0 copy-start.1
  104.9 0.0 copy-start.2
  104.9 0.0 reduce-scatter.2.cloned.1.call-update
  104.9 0.0 all-gather.4.cloned.1.call-start
  105.0 1.2 fusion.10
  106.2 0.0 copy-done.1
  106.3 0.0 copy-done.2
  106.3 83.0 %reduce-scatter.2.cloned.1.call-done = f32[64,2048]{1,0:T(8,128)} async-done(((f32[1024,2048]{1,0:T(8,128)}), f32[64,2048]{1,0:T(8,128)}) %reduce-scatter.2.cloned.1.call-update) | async-done | bytes 524304 | tf_op jit(solution)/shard_map/reduce_scatter | solution.py:545
  189.3 1.4 fusion.4
  190.7 1.3 collective-permute-start
  192.0 9.9 %collective-permute-done = f32[64,2048]{1,0:T(8,128)S(1)} collective-permute-done((f32[64,2048]{1,0:T(8,128)S(1)}, f32[64,2048]{1,0:T(8,128)S(1)}, u32[]{:S(2)}, u32[]{:S(2)}) %collective-permute-start) | collective-permute-done | bytes 524320 | tf_op jit(solution)/shard_map/ppermute | solution.py:540
  201.9 0.0 copy-start
  201.9 0.8 copy-done
  202.7 0.0 all-gather.4.cloned.1.call-update
  202.7 0.2 all-gather.6.cloned.1.call-start
  203.0 1.2 slice.27
  204.1 0.1 pad.3.clone
  204.2 0.5 iota_compare_fusion
  204.7 1.2 fusion.11
  205.9 0.9 maximum_maximum_fusion
  206.9 0.0 all-gather.6.cloned.1.call-update
  206.9 68.2 %all-gather.4.cloned.1.call-done.u_par = f32[1024,2048]{1,0:T(8,128)} async-done(((f32[64,2048]{1,0:T(8,128)}), f32[1024,2048]{1,0:T(8,128)}) %all-gather.4.cloned.1.call-update) | async-done | bytes 8388624 | tf_op jit(solution)/shard_map/all_gather | solution.py:540
  275.1 162.4 %head_grad.1 = f32[256,6400]{1,0:T(8,128)} custom-call(bf16[1024,2048]{1,0:T(8,128)(2,1)} %get-tuple-element.13.u_own, f32[1024,2048]{1,0:T(8,128)} %all-gather.4.cloned.1.call-done.u_par, f32[1024,6400]{1,0:T(8,128)} %get-tuple-element.11.z, bf16[2048,6400]{1,0:T(8,128)(2,1)} %w.5, f32[2,8,1024]{2,1,0:T(8,128)} %get-tuple-element.12.st, ...), custom_call_target="tpu_custom_call" | custom-call | flops 299999985664 | bytes 26214400 | tf_op jit(solution)/shard_map/head_grad/pallas_call | solution.py:456
  437.5 0.0 all-gather.6.cloned.1.call-done
  437.5 0.0 copy-start.3
  437.6 6.6 %convert.4 = bf16[16,72,2048]{2,1,0:T(8,128)(2,1)} convert(f32[16,72,2048]{2,1,0:T(8,128)} %bitcast.20) | non-fusion elementwise | flops 2359296 | bytes 14155776 | tf_op jit(solution)/shard_map/convert.1
  444.2 1.3 slice_reduce_fusion
  445.5 0.0 copy-done.3
  445.5 1.4 broadcast_select_fusion.part
  446.8 12.8 %dp_total.1 = f32[8,2048]{1,0:T(8,128)} custom-call(f32[8,2048]{1,0:T(8,128)} %broadcast_select_fusion.part), custom_call_target="tpu_custom_call" | custom-call | tf_op jit(solution)/shard_map/dp_total/pallas_call | solution.py:510
  459.6 1.5 fusion.13
  461.2 1.2 slice.29
  462.4 4.8 %fusion.12 = (bf16[8,64,2048]{2,1,0:T(8,128)(2,1)}, bf16[8,64,2048]{2,1,0:T(8,128)(2,1)}) fusion(bf16[16,72,2048]{2,1,0:T(8,128)(2,1)} %convert.4), kind=kLoop, calls=%fused_computation.25 | loop fusion | bytes 8388608 | tf_op jit(solution)/shard_map/slice | solution.py:556
  467.2 6.1 %copy.16 = f32[256,6400]{1,0:T(8,128)} copy(f32[256,6400]{1,0:T(8,128)} %head_grad.1) | data formatting | bytes 13107200
  (6 shorter events, 0.1 us)
Async XLA Ops:
  7.2 182.1 %reduce-scatter.2.cloned.1.call-start = ((), (), s32[]{:S(2)}) async-start(), calls=%async_computation.1 | async-start | bytes 8912896 | tf_op jit(solution)/shard_map/reduce_scatter | solution.py:545
  104.9 1.4 copy-start.1
  104.9 1.4 copy-start.2
  104.9 170.1 %all-gather.4.cloned.1.call-start = ((), (), s32[]{:S(2)}) async-start(), calls=%async_computation.2 | async-start | bytes 8912896 | tf_op jit(solution)/shard_map/all_gather | solution.py:540
  190.7 11.2 %collective-permute-start = (f32[64,2048]{1,0:T(8,128)S(1)}, f32[64,2048]{1,0:T(8,128)S(1)}, u32[]{:S(2)}, u32[]{:S(2)}) collective-permute-start(f32[64,2048]{1,0:T(8,128)S(1)} %convert_element_type.24), channel_id=1, source_target_pairs={{0,2},{1,3},{2,0},{3,1},{4,6},{5,7},{6,4},{7,5},{8,10},{9,11},{10,... | collective-permute-start | bytes 1572872 | tf_op jit(solution)/shard_map/ppermute | solution.py:540
  201.9 0.8 copy-start
  202.7 234.8 %all-gather.6.cloned.1.call-start = ((), (), s32[]{:S(2)}) async-start(), calls=%async_computation.3 | async-start | bytes 10027008 | tf_op jit(solution)/shard_map/all_gather | solution.py:551
  437.5 7.9 %copy-start.3 = (pred[8]{0:T(512)(128)(4,1)S(1)}, pred[8]{0:T(512)(128)(4,1)}, u32[]{:S(2)}) copy-start(pred[8]{0:T(512)(128)(4,1)} %iota_compare_fusion) | copy-start | bytes 28
Sparse Core Ops, SparseCore 0:
  105.1 84.1 reduce-scatter.1
  202.9 72.1 all-gather.3
  277.8 75.1 all-gather.5

commit v2 on v0

v2 whole, which is shorter than its diff:
```python
import functools

import jax
import jax.numpy as jnp
from jax import lax
from jax.experimental import pallas as pl
from jax.experimental.pallas import tpu as pltpu
from jax.sharding import PartitionSpec as P

NORM_EPS = 1e-6
MTP_LAMBDA = 0.3
MESH = pl.DeviceIdType.MESH
F32 = jnp.float32
BF16 = jnp.bfloat16
ANY = pl.BlockSpec(memory_space=pl.ANY)
VMEM = pl.BlockSpec(memory_space=pltpu.VMEM)


def columns(row, width=128):
    return jnp.broadcast_to(row, (width, row.shape[1])).T


RING = 4


class Torus:
    def __init__(self):
        self.tp, self.dp = lax.axis_index("tp"), lax.axis_index("dp")
        self.y, self.z = lax.rem(self.tp, RING), self.tp // RING
        self.x, self.core = self.dp // 2, lax.rem(self.dp, 2)
        self.mate = self.x + 1 - 2 * lax.rem(self.x, 2)
        self.far = 3 - self.x
        self.far_mate = self.far + 1 - 2 * lax.rem(self.far, 2)
        self.side = lax.rem((self.x + 1) // 2, 2)

    def chip(self, x, core):
        return {"tp": self.tp, "dp": 2 * x + core}

    def step(self, axis, d):
        y = lax.rem(self.y + d + RING, RING) if axis == 0 else self.y
        z = lax.rem(self.z + d + RING, RING) if axis == 1 else self.z
        return {"tp": z * RING + y, "dp": self.dp}

    def coords(self, s):
        return (0, self.y, 1, self.z) if s == 0 else (1, self.z, 0, self.y)


def greet(place, n_tp, n_dp):
    barrier = pltpu.get_barrier_semaphore()
    for d in range(1, n_tp):
        pl.semaphore_signal(barrier, inc=1, device_id={"tp": lax.rem(place.tp + d, n_tp), "dp": place.dp}, device_id_type=MESH)
    for d in range(1, n_dp):
        pl.semaphore_signal(barrier, inc=1, device_id={"tp": place.tp, "dp": lax.rem(place.dp + d, n_dp)}, device_id_type=MESH)
    return lambda: pl.semaphore_wait(barrier, n_tp + n_dp - 2)


def remote(src, dst, send, recv, to):
    return pltpu.make_async_remote_copy(src, dst, send, recv, device_id=to, device_id_type=MESH)


def arrived(dst, sem):
    pltpu.make_async_copy(dst, dst, sem).wait()


def ds(start, size, unit=8):
    return pl.ds(pl.multiple_of(start, unit), size)


def grad_logits(z, lse, rw, lab, col):
    lane = lax.broadcasted_iota(jnp.int32, z.shape, 1).astype(F32)
    p = jnp.exp(z - lse)
    return rw * jnp.where(lab - col == lane, p - 1.0, p)


LEFT = 4096
SLICE = 24
SPREAD = 2 * 16 * SLICE


def logits_kernel(n_tp, n_dp, chunk, left, hm, ht, gain_m, gain_t, lab_m, lab_t, wt_m, wt_t, w, z, u_out, up_out, du_out, st, lpart,
                  h_v, u_v, uf_v, got_v, w_v, z_v, e_v, x_v, m_v, s_v, t_v,
                  lab_v, send_v, land, wsend, wland, psend, pland, sem_h, sem_u, sem_w, sem_z, ssem, rsem, wssem, wrsem, pssem, prsem,
                  gs, gr, xs, xr, sem_d, sem_k):
    seq, depth = hm.shape
    rows, vocab = z.shape
    steps = vocab // chunk
    here = Torus()
    tp, dp = here.tp, here.dp
    mate = here.chip(here.mate, here.core)
    lo, hi = pl.ds(0, depth // 2), pl.ds(depth // 2, depth // 2)

    loads = [pltpu.make_async_copy(src, h_v.at[pl.ds(i * seq, seq), :], sem_h.at[i]) for i, src in enumerate((hm, ht))]

    def w_copy(i, slot):
        return pltpu.make_async_copy(w.at[:, ds(i * chunk, chunk, 128)], w_v.at[slot], sem_w.at[slot])

    def z_copy(i, slot):
        return pltpu.make_async_copy(z_v.at[slot], z.at[:, ds(i * chunk, chunk, 128)], sem_z.at[slot])

    for c in loads:
        c.start()
    w_copy(0, 0).start()
    met = greet(here, n_tp, n_dp)

    m_v[...] = jnp.full_like(m_v, -jnp.inf)
    s_v[...] = jnp.zeros_like(s_v)
    t_v[...] = jnp.zeros_like(t_v)
    first = (tp * vocab).astype(F32)
    lab_v[pl.ds(0, seq), :] = columns(lab_m[...].astype(F32) - first)
    lab_v[pl.ds(seq, seq), :] = columns(lab_t[...].astype(F32) - first)
    wrow = lax.broadcasted_iota(jnp.int32, (8, 128), 0)
    wsend[...] = jnp.where(wrow == 0, jnp.sum(wt_m[...]), jnp.sum(wt_t[...]))
    wland[dp] = wsend[...]

    for half, gain in ((0, gain_m), (1, gain_t)):
        loads[half].wait()
        g = gain[...]

        @pl.loop(0, seq // 128)
        def _(i):
            r = ds(half * seq + i * 128, 128, 128)
            x = h_v[r, :].astype(F32)
            inv = lax.rsqrt(jnp.mean(x * x, axis=-1, keepdims=True) + NORM_EPS)
            u = (x * inv * g).astype(BF16)
            u_v[r, :] = u
            uf_v[r, :] = u.astype(F32)

    u_copy = pltpu.make_async_copy(u_v, u_out, sem_u)
    u_copy.start()
    with jax.named_scope('meet'):
        met()

    def block(s, p1, p2):
        return ds(s * (SPREAD // 2) + (lax.rem(p2 + RING, RING) * RING + lax.rem(p1 + RING, RING)) * SLICE, SLICE)

    def group(s, p2):
        return ds(s * (SPREAD // 2) + lax.rem(p2 + RING, RING) * RING * SLICE, RING * SLICE)

    def hop(s, j, rows_of, lanes, axis, d):
        ref = got_v.at[rows_of, lanes]
        return remote(ref, ref, gs.at[s, j], gr.at[s, j], here.step(axis, d))

    def first_step(s):
        a1, p1, a2, p2 = here.coords(s)
        b = block(s, p1, p2)
        return [remote(uf_v.at[b, :], got_v.at[b, :], gs.at[s, 0], gr.at[s, 0], mate)]

    every = pl.ds(0, depth)

    def hops(s, stage):
        a1, p1, a2, p2 = here.coords(s)
        if stage == 1:
            b = block(s, p1, p2)
            return [hop(s, 1, b, every, a1, 1), hop(s, 2, b, every, a1, -1)]
        if stage == 2:
            return [hop(s, 3, block(s, p1 - 1, p2), lo, a1, 1), hop(s, 4, block(s, p1 + 1, p2), hi, a1, -1)]
        if stage == 3:
            return [hop(s, 5, group(s, p2), lo, a2, 1), hop(s, 6, group(s, p2), lo, a2, -1)]
        if stage == 4:
            return [hop(s, 9, group(s, p2), hi, a2, 1), hop(s, 10, group(s, p2), hi, a2, -1)]
        if stage == 5:
            return [hop(s, 7, group(s, p2 - 1), lo, a2, 1)]
        return [hop(s, 8, group(s, p2 + 1), hi, a2, -1)]

    def landed(s, stage):
        a1, p1, a2, p2 = here.coords(s)
        waits = {
            1: [(block(s, p1, p2), every, 0)],
            2: [(block(s, p1 - 1, p2), every, 1), (block(s, p1 + 1, p2), every, 2)],
            3: [(block(s, p1 - 2, p2), lo, 3), (block(s, p1 + 2, p2), hi, 4)],
            4: [],
            5: [(group(s, p2 - 1), lo, 5)],
            6: [(group(s, p2 + 1), hi, 10)],
            7: [(group(s, p2 + 1), lo, 6), (group(s, p2 - 1), hi, 9), (group(s, p2 - 2), lo, 7), (group(s, p2 + 2), hi, 8)],
        }
        for r, lanes, j in waits[stage]:
            arrived(got_v.at[r, lanes], gr.at[s, j])

    def pass_on(s, stage):
        landed(s, stage)
        for c in hops(s, stage):
            c.start()

    straight = remote(uf_v.at[pl.ds(SPREAD, rows - SPREAD), :], got_v.at[pl.ds(SPREAD, rows - SPREAD), :], xs, xr, mate)
    wcopies = []
    for d in range(1, n_dp):
        peer = lax.rem(dp + d, n_dp)
        c = remote(wsend, wland.at[dp], wssem.at[d], wrsem.at[dp], {"tp": tp, "dp": peer})
        c.start()
        wcopies.append(c)
    for c in first_step(0) + first_step(1) + [straight]:
        c.start()
    when = {(1, 0): (0, 1), (1, 3): (1, 1), (2, 0): (0, 2), (2, 3): (1, 2), (3, 0): (0, 3), (3, 3): (1, 3)}
    lane = lax.broadcasted_iota(jnp.int32, (rows, 128), 1).astype(F32)

    @pl.loop(0, steps)
    def _(i):
        slot = lax.rem(i, 2)
        with jax.named_scope('wwait'):
            w_copy(i, slot).wait()

        @pl.when(i + 1 < steps)
        def _():
            w_copy(i + 1, 1 - slot).start()

        @pl.when(i >= 2)
        def _():
            z_copy(i - 2, slot).wait()

        m, s, t = m_v[...], s_v[...], t_v[...]
        rel = lab_v[...] - (i * chunk).astype(F32)
        for n in range(chunk // 256):
            for (at_i, at_n), (which, stage) in when.items():
                if at_n == n:
                    @pl.when(i == at_i)
                    def _():
                        with jax.named_scope(f'pass{which}{stage}'):
                            pass_on(which, stage)
            cols = slice(n * 256, (n + 1) * 256)
            zz = jnp.dot(u_v[...], w_v[slot, :, cols], preferred_element_type=F32)
            z_v[slot, :, cols] = zz
            za, zb = zz[:, :128], zz[:, 128:]
            new = jnp.maximum(m, jnp.maximum(za, zb))
            s = s * jnp.exp(m - new) + (jnp.exp(za - new) + jnp.exp(zb - new))
            t = jnp.where(rel == lane + n * 256, za, t)
            t = jnp.where(rel == lane + (n * 256 + 128), zb, t)
            m = new
        m_v[...], s_v[...], t_v[...] = m, s, t
        z_copy(i, slot).start()

    mt = m_v[...].T
    top = jnp.max(mt, axis=0, keepdims=True)
    total = jnp.sum(s_v[...].T * jnp.exp(mt - top), axis=0, keepdims=True)
    hit = jnp.sum(t_v[...].T, axis=0, keepdims=True)
    mine = jnp.where(lax.broadcasted_iota(jnp.int32, (2, rows), 0) == 0, top + jnp.log(total), hit)
    send_v[...] = mine
    land[tp] = mine
    copies = []
    for d in range(1, n_tp):
        peer = lax.rem(tp + d, n_tp)
        c = remote(send_v, land.at[tp], ssem.at[d], rsem.at[tp], {"tp": peer, "dp": dp})
        c.start()
        copies.append(c)
    with jax.named_scope('pass45'):
        for stage in (4, 5):
            for which in range(2):
                pass_on(which, stage)
    for d in range(1, n_dp):
        src = lax.rem(dp + d, n_dp)
        arrived(wland.at[src], wrsem.at[src])
    sums = wland[0]
    for d in range(1, n_dp):
        sums = sums + wland[d]
    coef_m = 1.0 / sums[0:1, 0:1]
    coef_t = MTP_LAMBDA / sums[1:2, 0:1]
    rw = jnp.concatenate([wt_m[...] * coef_m, wt_t[...] * coef_t], axis=1)
    lab = jnp.concatenate([lab_m[...], lab_t[...]], axis=1).astype(F32)
    with jax.named_scope('statwait'):
        for d in range(1, n_tp):
            src = lax.rem(tp + d, n_tp)
            arrived(land.at[src], rsem.at[src])
    top = land[0]
    for d in range(1, n_tp):
        top = jnp.maximum(top, land[d])
    acc = jnp.zeros_like(top)
    hits = jnp.zeros_like(top)
    for d in range(n_tp):
        acc = acc + jnp.exp(land[d] - top)
        hits = hits + land[d]
    lse = (top + jnp.log(acc))[0:1, :]
    hit = hits[1:2, :]
    lpart[...] = jnp.broadcast_to(jnp.sum(rw * (lse - hit)), (8, 128))
    srow = lax.broadcasted_iota(jnp.int32, (8, rows), 0)
    mine = jnp.where(srow == 0, lse, jnp.where(srow == 1, rw, lab - first))
    psend[...] = mine
    st[0] = mine
    swap = remote(psend, pland, pssem, prsem, mate)
    swap.start()
    m_v[...] = columns(lse)
    s_v[...] = columns(rw)

    skip = left - (steps - 2) * chunk
    for step, begin, at in ((steps - 1, 0, 0), (steps - 2, skip, chunk)):
        for c in range(begin, chunk, 128):
            e_v[:, at + c - begin:at + c - begin + 128] = grad_logits(
                z_v[step % 2, :, c:c + 128], m_v[...], s_v[...], lab_v[...], float(step * chunk + c)).astype(BF16)

    def e_dot(r, n):
        cols = slice(n * 512, (n + 1) * 512)
        nt = (((1,), (1,)), ((), ()))
        return (lax.dot_general(e_v[r, :chunk], w_v[(steps - 1) % 2, cols, :], nt, preferred_element_type=F32)
                + lax.dot_general(e_v[r, chunk:], w_v[(steps - 2) % 2, cols, skip:], nt, preferred_element_type=F32))

    def du_copy(part, n):
        cols = pl.ds(n * 512, 512)
        src, r = ((uf_v.at[pl.ds(0, SPREAD), cols], pl.ds(0, SPREAD)), (x_v.at[:, cols], pl.ds(SPREAD, rows - SPREAD)))[part]
        return pltpu.make_async_copy(src, du_out.at[r, cols], sem_d.at[part, n])

    with jax.named_scope('sendwait'):
        for c in first_step(0) + first_step(1):
            c.wait_send()
    for n in range(depth // 512):
        cols = slice(n * 512, (n + 1) * 512)
        uf_v[:SPREAD, cols] = e_dot(slice(0, SPREAD), n)
        du_copy(0, n).start()
        if n == 1:
            with jax.named_scope('pass06'):
                pass_on(0, 6)
        if n == 2:
            with jax.named_scope('pass16'):
                pass_on(1, 6)
    for n in range(depth // 512):
        cols = slice(n * 512, (n + 1) * 512)
        x_v[:, cols] = e_dot(slice(SPREAD, rows), n)
        du_copy(1, n).start()
    u_copy.wait()
    with jax.named_scope('swapwait'):
        swap.wait()
    st[1] = pland[...]

    def keep(i, begin, end):
        @pl.loop(begin // 128, end // 128)
        def _(j):
            r = ds(j * 128, 128, 128)
            u_v[r, :] = got_v[r, :].astype(BF16)
        return pltpu.make_async_copy(u_v.at[pl.ds(begin, end - begin), :], up_out.at[pl.ds(begin, end - begin), :], sem_k.at[i])

    kept = []
    parts = [(0, SPREAD // 2, lambda: landed(0, 7)), (SPREAD // 2, SPREAD, lambda: landed(1, 7)),
             (SPREAD, rows, lambda: arrived(got_v.at[pl.ds(SPREAD, rows - SPREAD), :], xr))]
    for i, (begin, end, wait) in enumerate(parts):
        with jax.named_scope(f'land{i}'):
            wait()
        kept.append(keep(i, begin, end))
        kept[-1].start()
    tail = jax.named_scope('tail')
    tail.__enter__()
    for c in wcopies + copies:
        c.wait_send()
    for s in range(2):
        for stage in range(1, 7):
            for c in hops(s, stage):
                c.wait_send()
    z_copy(steps - 2, (steps - 2) % 2).wait()
    z_copy(steps - 1, (steps - 1) % 2).wait()
    straight.wait_send()
    for n in range(depth // 512):
        for part in range(2):
            du_copy(part, n).wait()
    for c in kept:
        c.wait()
    tail.__exit__(None, None, None)


def logits(n_tp, n_dp, hm, ht, gain_m, gain_t, lab_m, lab_t, wt_m, wt_t, w):
    seq, depth = hm.shape
    rows, vocab = 2 * seq, w.shape[1]
    chunk = 1280
    dma = pltpu.SemaphoreType.DMA
    return pl.pallas_call(
        functools.partial(logits_kernel, n_tp, n_dp, chunk, LEFT),
        out_shape=(
            jax.ShapeDtypeStruct((rows, vocab), F32),
            jax.ShapeDtypeStruct((rows, depth), BF16),
            jax.ShapeDtypeStruct((rows, depth), BF16),
            jax.ShapeDtypeStruct((rows, depth), F32),
            jax.ShapeDtypeStruct((2, 8, rows), F32),
            jax.ShapeDtypeStruct((8, 128), F32),
        ),
        in_specs=[ANY, ANY] + [VMEM] * 6 + [ANY],
        out_specs=(ANY, ANY, ANY, ANY, VMEM, VMEM),
        scratch_shapes=[
            pltpu.VMEM((rows, depth), BF16),
            pltpu.VMEM((rows, depth), BF16),
            pltpu.VMEM((rows, depth), F32),
            pltpu.VMEM((rows, depth), F32),
            pltpu.VMEM((2, depth, chunk), BF16),
            pltpu.VMEM((2, rows, chunk), F32),
            pltpu.VMEM((rows, vocab - LEFT), BF16),
            pltpu.VMEM((rows - SPREAD, depth), F32),
            pltpu.VMEM((rows, 128), F32),
            pltpu.VMEM((rows, 128), F32),
            pltpu.VMEM((rows, 128), F32),
            pltpu.VMEM((rows, 128), F32),
            pltpu.VMEM((2, rows), F32),
            pltpu.VMEM((n_tp, 2, rows), F32),
            pltpu.VMEM((8, 128), F32),
            pltpu.VMEM((n_dp, 8, 128), F32),
            pltpu.VMEM((8, rows), F32),
            pltpu.VMEM((8, rows), F32),
            dma((2,)), dma, dma((2,)), dma((2,)),
            dma((n_tp,)), dma((n_tp,)), dma((n_dp,)), dma((n_dp,)), dma, dma,
            dma((2, 11)), dma((2, 11)), dma, dma, dma((2, depth // 512)), dma((3,)),
        ],
        compiler_params=pltpu.CompilerParams(vmem_limit_bytes=67043328, collective_id=0, has_side_effects=True),
        cost_estimate=pl.CostEstimate(flops=2 * rows * depth * vocab, bytes_accessed=2 * depth * vocab, transcendentals=0),
        name="logits",
    )(hm, ht, gain_m, gain_t, lab_m, lab_t, wt_m, wt_t, w)


def head_kernel(n_tp, n_dp, first, wide, task, left, plan, hm, ht, gain_m, gain_t, u_own, u_par, z, w, st, du_in, lpart,
                fin, gh, ghb, du, tot, u_v, w_v, z_v, et_v, g_v, own_v, sum_v, one_v, acc_v, e_v,
                lse_v, rw_v, lab_v, ra_v, rl_v, rb_v, rm_v, ra2_v, rb2_v, rh_v, gg_v, gland, tland, tsend,
                sem_u, sem_p, sem_w, sem_z, sem_a, sem_o, d_send, d_recv, b_send, b_recv, f_send, f_recv,
                rs, rr, sem_l, sem_x, g_s, g_r, t_s, t_r):
    rows, depth = u_own.shape
    seq = rows // 2
    vocab = z.shape[1]
    half = vocab // 2
    here = Torus()
    tp, dp = here.tp, here.dp
    x, core, side, mate, far, far_mate = here.x, here.core, here.side, here.mate, here.far, here.far_mate
    met = greet(here, n_tp, n_dp)

    blocks = [2 * j + 1 - core for j in range(4)] + [2 * j + core for j in range(4)]
    block = [ds(b * 256, 256, 256) for b in blocks]

    def u_copies(k):
        return [pltpu.make_async_copy((u_own, u_par)[k].at[:, block[i]], u_v.at[pl.ds(k * rows, rows), pl.ds(i * 256, 256)], sem_u.at[k, i])
                for i in range(8)]

    def u_wait(k):
        with jax.named_scope('uwait'):
            for c in u_copies(k):
                c.wait()

    def w_copies(col, width, slot):
        return [pltpu.make_async_copy(w.at[block[i], ds(col, width, 128)],
                                      w_v.at[slot, pl.ds(i * 256, 256), pl.ds(0, width)], sem_w.at[slot, i]) for i in range(8)]

    def z_copy(col, width, slot):
        return pltpu.make_async_copy(z.at[:, ds(col, width, 128)], z_v.at[slot, :, pl.ds(0, width)], sem_z.at[slot])

    def fetch(c0, width, slot):
        for c in w_copies(side * half + c0, width, slot) + [z_copy(side * half + c0, width, slot)]:
            c.start()

    n = (half - first) // wide
    start = lambda k: pl.multiple_of(first + (k - 1) * wide, 128)
    fetch(0, first, 0)
    for c in u_copies(1):
        c.start()
    for k in range(2):
        r = pl.ds(k * rows, rows)
        lse_v[r, :] = columns(st[k, 0:1, :])
        rw_v[r, :] = columns(st[k, 1:2, :])
        lab_v[r, :] = columns(st[k, 2:3, :])
    def d_copy(k, c0, width, part):
        lanes = pl.ds(part * 512, 512)
        return remote(g_v.at[lax.rem(k, 2), pl.ds(0, width), lanes], sum_v.at[pl.ds(c0, width), lanes], d_send.at[lax.rem(k, 2), part],
                      d_recv.at[k, part], here.chip(x, 1 - core))

    def b_copy(k, c0, width, which):
        chip = (far_mate, far)[which]
        return remote(sum_v.at[pl.ds(c0, width), ds(chip * 256, 256, 256)], one_v.at[which, pl.ds(c0, width), :],
                      b_send.at[2 * k + which], b_recv.at[2 * k + which], here.chip(far, core))

    def f_copy(k, c0, width):
        return remote(sum_v.at[pl.ds(c0, width), ds(mate * 256, 256, 256)], fin.at[1, pl.ds(c0, width), :],
                      f_send.at[k], f_recv.at[k], here.chip(mate, core))

    def o_copy(k, c0, width):
        return pltpu.make_async_copy(sum_v.at[pl.ds(c0, width), ds(x * 256, 256, 256)], fin.at[0, pl.ds(c0, width), :], sem_o.at[k])

    def make(k, c0, width, slot, begin=lambda: None, early=lambda: None, middle=lambda: None):
        with jax.named_scope('wzwait'):
            for c in w_copies(side * half + c0, width, slot) + [z_copy(side * half + c0, width, slot)]:
                c.wait()
        begin()
        col = (side * half + c0).astype(F32)
        own, par = pl.ds(0, rows), pl.ds(rows, rows)
        for g in range(width // 128):
            cols = slice(g * 128, (g + 1) * 128)
            e = grad_logits(z_v[slot, :, cols], lse_v[own, :], rw_v[own, :], lab_v[own, :], col + g * 128)
            et_v[cols, own] = e.T.astype(BF16)
        early()
        for n in range(0, width, 256):
            step = min(width - n, 256)
            zz = jnp.dot(u_v[par, :], w_v[slot, :, n:n + step], preferred_element_type=F32)
            for c1 in range(n, n + step, 128):
                e = grad_logits(zz[:, c1 - n:c1 - n + 128], lse_v[par, :], rw_v[par, :], lab_v[par, :], col + c1)
                et_v[c1:c1 + 128, par] = e.T.astype(BF16)
        middle()
        et = et_v[pl.ds(0, width), :]
        for part in range(2):
            g_v[lax.rem(k, 2), pl.ds(0, width), part * 512:(part + 1) * 512] = jnp.dot(et, u_v[:, part * 512:(part + 1) * 512], preferred_element_type=F32)
            d_copy(k, c0, width, part).start()
        own_v[pl.ds(0, width), :] = jnp.dot(et, u_v[:, 1024:], preferred_element_type=F32)

    def add(k, c0, width):
        with jax.named_scope('dwait'):
            for part in range(2):
                d_copy(k, c0, width, part).wait_recv()
        r = pl.ds(c0, width)
        sum_v[r, :] += own_v[pl.ds(0, width), :]
        for which in range(2):
            b_copy(k, c0, width, which).start()

    def close(k, c0, width):
        r = pl.ds(c0, width)
        for which, chip in enumerate((mate, x)):
            with jax.named_scope('bwait'):
                b_copy(k, c0, width, which).wait_recv()
            sum_v[r, ds(chip * 256, 256, 256)] += one_v[which, r, :]
            (f_copy if which == 0 else o_copy)(k, c0, width).start()

    per = left // task

    def acc_copies(h, back):
        out = []
        for i in range(8):
            mine, there = acc_v.at[:, pl.ds(i * 256, 256)], (du if back else du_in).at[ds(h * seq, seq, 256), block[i]]
            out.append(pltpu.make_async_copy(*((mine, there) if back else (there, mine)), sem_a.at[i]))
        return out

    def du_fetch(t, slot):
        h, i = t // per, lax.rem(t, per)
        for c in w_copies(i * task, task, slot):
            c.start()
        pltpu.make_async_copy(z.at[ds(h * seq, seq, 256), ds(i * task, task, 128)], z_v.at[slot, pl.ds(0, seq), :], sem_z.at[slot]).start()

    def du_wait(slot):
        for c in w_copies(0, task, slot):
            c.wait()
        pltpu.make_async_copy(z.at[pl.ds(0, seq), pl.ds(0, task)], z_v.at[slot, pl.ds(0, seq), :], sem_z.at[slot]).wait()

    def du_run(k, lo, hi):
        @pl.loop(lo, hi)
        def _(t):
            slot = lax.rem(k + 1 + t, 2)
            h, i = t // per, lax.rem(t, per)
            at_point(t, "task")

            @pl.when(t + 1 < hi)
            def _():
                du_fetch(t + 1, 1 - slot)

            @pl.when((t + 1 == hi) & (k < n))
            def _():
                fetch(start(k + 1), wide, 1 - slot)

            du_wait(slot)

            @pl.when(i == 0)
            def _():
                for c in acc_copies(h, False):
                    c.wait()

            r = ds(h * seq, seq, 256)
            col = (i * task).astype(F32)
            for g in range(task // 128):
                cols = slice(g * 128, (g + 1) * 128)
                e_v[:, cols] = grad_logits(z_v[slot, :seq, cols], lse_v[r, :], rw_v[r, :], lab_v[r, :], col + g * 128).astype(BF16)
            for m in range(depth // 512):
                cols = slice(m * 512, (m + 1) * 512)
                acc_v[:, cols] += lax.dot_general(e_v[...], w_v[slot, cols, :], (((1,), (1,)), ((), ())), preferred_element_type=F32)

            @pl.when(i == per - 1)
            def _():
                acc_v[...] = acc_v[...].astype(BF16).astype(F32)
                for c in acc_copies(h, True):
                    c.start()
                for c in acc_copies(h, True):
                    c.wait()

            @pl.when((i == per - 1) & (h == 0))
            def _():
                for c in acc_copies(1, False):
                    c.start()

    lo, hi, every = pl.ds(0, depth // 2), pl.ds(depth // 2, depth // 2), pl.ds(0, depth)

    def mod(p):
        return lax.rem(p + RING, RING)

    def ring(h, s):
        q = 2 * h + s
        a1, p1, a2, p2 = here.coords(s)
        base = h * seq + s * (seq // 2)

        def rows1(p):
            return ds(base + mod(p) * 64, 64, 64)

        def rows2(p):
            return ds(base + p1 * 64 + mod(p) * 16, 16, 16)

        def sub(p):
            return ds(mod(p) * 16, 16, 16)

        def go(j, src, dst, axis, d):
            return lambda: remote(src, dst, rs.at[q, j], rr.at[q, j], here.step(axis, d))

        def near(src, dst, j):
            return lambda: pltpu.make_async_copy(src, dst, sem_l.at[q, j])

        sends = {
            0: [go(0, du.at[rows1(p1 + 2), lo], ra_v.at[q, 0], a1, 1), go(1, du.at[rows1(p1 + 2), hi], ra_v.at[q, 1], a1, -1),
                go(2, du.at[rows1(p1 + 1), hi], rb_v.at[q, 0, :, hi], a1, 1), go(3, du.at[rows1(p1 - 1), lo], rb_v.at[q, 1, :, lo], a1, -1)],
            1: [go(4, ra_v.at[q, 0], rb_v.at[q, 0, :, lo], a1, 1), go(5, ra_v.at[q, 1], rb_v.at[q, 1, :, hi], a1, -1)],
            2: [go(6, rm_v.at[q, sub(p2 + 2), lo], ra2_v.at[q, 0], a2, 1), go(7, rm_v.at[q, sub(p2 + 2), hi], ra2_v.at[q, 1], a2, -1),
                go(8, rm_v.at[q, sub(p2 + 1), hi], rb2_v.at[q, 0, :, hi], a2, 1), go(9, rm_v.at[q, sub(p2 - 1), lo], rb2_v.at[q, 1, :, lo], a2, -1)],
            3: [go(10, ra2_v.at[q, 0], rb2_v.at[q, 0, :, lo], a2, 1), go(11, ra2_v.at[q, 1], rb2_v.at[q, 1, :, hi], a2, -1)],
            4: [go(12, rm_v.at[q, sub(p2), :], gh.at[rows2(p2), :], a2, 1), go(13, rm_v.at[q, sub(p2), :], gh.at[rows2(p2), :], a2, -1)],
            5: [go(14, gh.at[rows2(p2 - 1), lo], gh.at[rows2(p2 - 1), lo], a2, 1), go(15, gh.at[rows2(p2 + 1), hi], gh.at[rows2(p2 + 1), hi], a2, -1)],
            6: [go(16, gh.at[rows1(p1), :], gh.at[rows1(p1), :], a1, 1), go(17, gh.at[rows1(p1), :], gh.at[rows1(p1), :], a1, -1)],
            7: [go(18, gh.at[rows1(p1 - 1), lo], gh.at[rows1(p1 - 1), lo], a1, 1), go(19, gh.at[rows1(p1 + 1), hi], gh.at[rows1(p1 + 1), hi], a1, -1)],
        }
        lands = {
            0: [(ra_v.at[q, 0], 0), (ra_v.at[q, 1], 1)],
            1: [(rb_v.at[q, 0, :, hi], 2), (rb_v.at[q, 1, :, lo], 3), (rb_v.at[q, 0, :, lo], 4), (rb_v.at[q, 1, :, hi], 5)],
            2: [(ra2_v.at[q, 0], 6), (ra2_v.at[q, 1], 7)],
            3: [(rb2_v.at[q, 0, :, hi], 8), (rb2_v.at[q, 1, :, lo], 9), (rb2_v.at[q, 0, :, lo], 10), (rb2_v.at[q, 1, :, hi], 11)],
            4: [(gh.at[rows2(p2 - 1), :], 12), (gh.at[rows2(p2 + 1), :], 13)],
            5: [(gh.at[rows2(p2 - 2), lo], 14), (gh.at[rows2(p2 + 2), hi], 15)],
            6: [(gh.at[rows1(p1 - 1), :], 16), (gh.at[rows1(p1 + 1), :], 17)],
            7: [(gh.at[rows1(p1 - 2), lo], 18), (gh.at[rows1(p1 + 2), hi], 19)],
        }
        local = [near(du.at[rows1(p1 + 1), lo], rl_v.at[s, 0], 0), near(du.at[rows1(p1 - 1), hi], rl_v.at[s, 1], 1),
                 near(du.at[rows1(p1), :], rm_v.at[q], 2),
                 near((hm, ht)[h].at[ds(s * (seq // 2) + p1 * 64 + p2 * 16, 16, 16), :], rh_v.at[q], 3)]

        def keep():
            return pltpu.make_async_copy(rm_v.at[q, sub(p2), :], gh.at[rows2(p2), :], sem_x.at[q])

        return q, sub, p2, sends, lands, local, keep

    def event(h, stage):
        for s in range(2):
            q, sub, p2, sends, lands, local, keep = ring(h, s)
            if stage == 0:
                for c in sends[0] + local:
                    c().start()
                continue
            if stage == 1:
                for c in local:
                    c().wait()
            if stage == 6:
                keep().wait()
            for ref, j in lands[stage - 1]:
                arrived(ref, rr.at[q, j])
            if stage == 1:
                ra_v[q] += rl_v[s]
            if stage == 2:
                rm_v[q] += rb_v[q, 0] + rb_v[q, 1]
            if stage == 3:
                ra2_v[q, 0] += rm_v[q, sub(p2 + 1), lo]
                ra2_v[q, 1] += rm_v[q, sub(p2 - 1), hi]
            if stage == 4:
                gu = rm_v[q, sub(p2), :] + (rb2_v[q, 0] + rb2_v[q, 1])
                xr = rh_v[q].astype(F32)
                inv = lax.rsqrt(jnp.mean(xr * xr, axis=-1, keepdims=True) + NORM_EPS)
                normed = xr * inv
                gn = gu * (gain_m, gain_t)[h][...]
                gx = inv * (gn - normed * jnp.mean(gn * normed, axis=-1, keepdims=True))
                rm_v[q, sub(p2), :] = gx.astype(BF16).astype(F32)
                part = jnp.sum(gu * normed, axis=0, keepdims=True)
                if s == 0:
                    gg_v[h:h + 1, :] = part
                else:
                    gg_v[h:h + 1, :] += part
                keep().start()
            if stage < 8:
                for c in sends[stage]:
                    c().start()

    def narrow(h):
        r = pl.ds(h * seq, seq)
        c = pltpu.make_async_copy(gh.at[r, :], acc_v, sem_a.at[0])
        c.start()
        c.wait()
        u_v[r, :] = acc_v[...].astype(BF16)
        pltpu.make_async_copy(u_v.at[r, :], ghb.at[r, :], sem_u.at[0, h]).start()

    def g_copy(d):
        return remote(gg_v, gland.at[tp], g_s.at[d], g_r.at[tp], {"tp": lax.rem(tp + d, n_tp), "dp": dp})

    def t_copy(d):
        return remote(tsend, tland.at[dp], t_s.at[d], t_r.at[dp], {"tp": tp, "dp": lax.rem(dp + d, n_dp)})

    def gains(stage):
        if stage == 0:
            gland[tp] = gg_v[...]
            for d in range(1, n_tp):
                g_copy(d).start()
        if stage == 1:
            for d in range(1, n_tp):
                src = lax.rem(tp + d, n_tp)
                arrived(gland.at[src], g_r.at[src])
            total = gland[0]
            for d in range(1, n_tp):
                total = total + gland[d]
            total = jnp.concatenate([total, jnp.broadcast_to(lpart[0:1, 0:1], total.shape)])
            tsend[...] = total
            tland[dp] = total
            for d in range(1, n_dp):
                t_copy(d).start()
        if stage == 2:
            for d in range(1, n_dp):
                src = lax.rem(dp + d, n_dp)
                arrived(tland.at[src], t_r.at[src])
            total = tland[0]
            for d in range(1, n_dp):
                total = total + tland[d]
            tot[...] = total

    gg_v[...] = jnp.zeros_like(gg_v)

    def where(k):
        return (0, first) if isinstance(k, int) and k == 0 else (start(k), wide)

    def drain():
        for h in range(2):
            for s in range(2):
                for cs in ring(h, s)[3].values():
                    for c in cs:
                        c().wait_send()
        for d in range(1, n_tp):
            g_copy(d).wait_send()
        for d in range(1, n_dp):
            t_copy(d).wait_send()
        for k in range(n):
            c0, width = where(k)
            if k < n - 1:
                f_copy(k, c0, width).wait()
                o_copy(k, c0, width).wait()
            for which in range(2):
                b_copy(k, c0, width, which).wait_send()
            if k >= n - 1:
                for part in range(2):
                    d_copy(k, c0, width, part).wait_send()

    def act(what, *args):
        with jax.named_scope(what + "".join(str(a) for a in args)):
            {"ring": event, "sums": gains, "narrow": narrow, "drain": drain, "add": lambda k: add(k, *where(k)), "close": lambda k: close(k, *where(k))}[what](*args)

    def pick(table, k, default):
        out = jnp.int32(default)
        for at_k, value in table.items():
            out = jnp.where(k == at_k, value, out)
        return out

    def at_point(k, point):
        for (at_k, at_p), todo in plan["acts"].items():
            if at_p == point:
                @pl.when(k == at_k)
                def _():
                    for a in todo:
                        act(*a)

    def more_loads():
        for c in u_copies(0):
            c.start()
        fetch(start(1), wide, 1)
        for c in acc_copies(0, False):
            c.start()

    def before_sends():
        u_wait(0)
        with jax.named_scope('meet'):
            met()

    with jax.named_scope('make0'):
        make(0, 0, first, 0, more_loads, lambda: u_wait(1), before_sends)
    add(0, 0, first)

    @pl.loop(1, n + 1)
    def _(k):
        lo_t = pick({a: v[0] for a, v in plan["du"].items()}, k, 2 * per)
        hi_t = pick({a: v[1] for a, v in plan["du"].items()}, k, 2 * per)
        before = pick(plan["before"], k, 2 * per)
        slot = lax.rem(k + before, 2)

        @pl.when(hi_t > lo_t)
        def _():
            du_fetch(lo_t, 1 - slot)

        @pl.when((hi_t == lo_t) & (k < n))
        def _():
            fetch(start(k + 1), wide, 1 - slot)

        @pl.when(k == 2)
        def _():
            for part in range(2):
                d_copy(0, 0, first, part).wait_send()

        @pl.when(k > 2)
        def _():
            for part in range(2):
                d_copy(k - 2, start(k - 2), wide, part).wait_send()

        with jax.named_scope('make'):
            make(k, start(k), wide, slot, middle=lambda: at_point(k, "middle"))

        @pl.when(k < n)
        def _():
            add(k, start(k), wide)

        at_point(k, "add")
        with jax.named_scope('du_run'):
            du_run(k, lo_t, hi_t)
        at_point(k, "du")
        done = pick(plan["close"], k, -1)

        @pl.when(done == 0)
        def _():
            close(0, 0, first)

        @pl.when(done > 0)
        def _():
            close(done, start(done), wide)

        at_point(k, "close")

    for a in plan["tail"]:
        act(*a)
    tail = jax.named_scope('tail')
    tail.__enter__()
    for k in (n - 1, n):
        c0, width = where(k)
        f_copy(k, c0, width).wait()
        o_copy(k, c0, width).wait()
    for which in range(2):
        b_copy(n, start(n), wide, which).wait_send()
    for part in range(2):
        d_copy(n, start(n), wide, part).wait_send()
    for h in range(2):
        r = pl.ds(h * seq, seq)
        pltpu.make_async_copy(u_v.at[r, :], ghb.at[r, :], sem_u.at[0, h]).wait()
    tail.__exit__(None, None, None)


PLAN = {
    "du": {2: (0, 8), 3: (8, 12), 4: (12, 16)},
    "before": {1: 0, 2: 0, 3: 8, 4: 12},
    "close": {2: 0, 3: 1, 4: 2, 5: 3, 7: 4},
    "acts": {
        (2, "du"): [("ring", 0, 0)], (3, "du"): [("ring", 0, 1)], (4, "add"): [("ring", 0, 2)], (14, "task"): [("ring", 0, 3)],
        (4, "du"): [("ring", 0, 4), ("ring", 1, 0)], (5, "middle"): [("ring", 0, 5)],
        (6, "middle"): [("ring", 1, 1), ("ring", 0, 6)], (7, "middle"): [("ring", 1, 2)], (7, "add"): [("ring", 1, 3)],
        (8, "middle"): [("ring", 1, 4)], (8, "add"): [("ring", 0, 7), ("ring", 1, 5)],
    },
    "tail": [("close", 5), ("sums", 0), ("ring", 1, 6), ("close", 6), ("sums", 1), ("add", 8), ("ring", 0, 8), ("narrow", 0), ("ring", 1, 7),
             ("close", 7), ("ring", 1, 8), ("narrow", 1), ("sums", 2), ("drain",), ("close", 8)],
}


def head_grad(n_tp, n_dp, hm, ht, gain_m, gain_t, u_own, u_par, z, w, st, du_in, lpart):
    rows, depth = u_own.shape
    vocab = z.shape[1]
    first, wide, task = 128, 384, 512
    half = vocab // 2
    n = (half - first) // wide + 1
    dma = pltpu.SemaphoreType.DMA
    return pl.pallas_call(
        functools.partial(head_kernel, n_tp, n_dp, first, wide, task, LEFT, PLAN),
        out_shape=(
            jax.ShapeDtypeStruct((2, half, 256), F32),
            jax.ShapeDtypeStruct((rows, depth), F32),
            jax.ShapeDtypeStruct((rows, depth), BF16),
            jax.ShapeDtypeStruct((rows, depth), F32),
            jax.ShapeDtypeStruct((4, depth), F32),
        ),
        in_specs=[ANY, ANY, VMEM, VMEM, ANY, ANY, ANY, ANY, VMEM, ANY, VMEM],
        out_specs=(ANY, ANY, ANY, ANY, VMEM),
        scratch_shapes=[
            pltpu.VMEM((2 * rows, depth), BF16),
            pltpu.VMEM((2, depth, task), BF16),
            pltpu.VMEM((2, rows, task), F32),
            pltpu.VMEM((wide, 2 * rows), BF16),
            pltpu.VMEM((2, wide, 1024), F32),
            pltpu.VMEM((wide, 1024), F32),
            pltpu.VMEM((half, 1024), F32),
            pltpu.VMEM((2, half, 256), F32),
            pltpu.VMEM((rows // 2, depth), F32),
            pltpu.VMEM((rows // 2, task), BF16),
            pltpu.VMEM((2 * rows, 128), F32),
            pltpu.VMEM((2 * rows, 128), F32),
            pltpu.VMEM((2 * rows, 128), F32),
            pltpu.VMEM((4, 2, 64, depth // 2), F32),
            pltpu.VMEM((2, 2, 64, depth // 2), F32),
            pltpu.VMEM((4, 2, 64, depth), F32),
            pltpu.VMEM((4, 64, depth), F32),
            pltpu.VMEM((4, 2, 16, depth // 2), F32),
            pltpu.VMEM((4, 2, 16, depth), F32),
            pltpu.VMEM((4, 16, depth), BF16),
            pltpu.VMEM((2, depth), F32),
            pltpu.VMEM((n_tp, 2, depth), F32),
            pltpu.VMEM((n_dp, 4, depth), F32),
            pltpu.VMEM((4, depth), F32),
            dma((2, 8)), dma, dma((2, 8)), dma((2,)), dma((8,)), dma((n,)),
            dma((2, 2)), dma((n, 2)), dma((2 * n,)), dma((2 * n,)), dma((n,)), dma((n,)),
            dma((4, 20)), dma((4, 20)), dma((4, 4)), dma((4,)), dma((n_tp,)), dma((n_tp,)), dma((n_dp,)), dma((n_dp,)),
        ],
        compiler_params=pltpu.CompilerParams(vmem_limit_bytes=67043328, collective_id=1, has_side_effects=True),
        cost_estimate=pl.CostEstimate(flops=300 * 10**9, bytes_accessed=2 * depth * vocab, transcendentals=0),
        name="head_grad",
    )(hm, ht, gain_m, gain_t, u_own, u_par, z, w, st, du_in, lpart)


def finish_kernel(span, fin, gh, tot, out, gm, gt, loss, ggm, ggt, f_v, o_v, g_v, sem_f, sem_o, sem_g, sem_b):
    half = fin.shape[1]
    seq = gm.shape[0]
    side = Torus().side
    nf, ng = 2 * half // span, gh.shape[0] // 128

    def f_in(i):
        k, j = divmod(i, half // span)
        return pltpu.make_async_copy(fin.at[k, pl.ds(j * span, span), :], f_v.at[i], sem_f.at[i])

    def f_out(i):
        k, j = divmod(i, half // span)
        col = (side if k == 0 else 1 - side) * half + j * span
        return pltpu.make_async_copy(o_v.at[i], out.at[:, ds(col, span, 128)], sem_o.at[i])

    def g_in(i):
        return pltpu.make_async_copy(gh.at[pl.ds(i * 128, 128), :], g_v.at[i], sem_g.at[i])

    def g_out(i):
        dst = (gm, gt)[i * 128 // seq]
        return pltpu.make_async_copy(g_v.at[i], dst.at[pl.ds(i * 128 % seq, 128), :], sem_b.at[i])

    for i in range(nf):
        f_in(i).start()
    for i in range(ng):
        g_in(i).start()
    loss[...] = tot[2:3, 0:1]
    ggm[...] = tot[0:1, :]
    ggt[...] = tot[1:2, :]
    for i in range(nf):
        f_in(i).wait()
        o_v[i] = f_v[i].T
        f_out(i).start()
    for i in range(ng):
        g_in(i).wait()
        g_out(i).start()
    for i in range(nf):
        f_out(i).wait()
    for i in range(ng):
        g_out(i).wait()


def finish(fin, gh, tot):
    _, half, block = fin.shape
    rows, depth = gh.shape
    span = 640
    nf, ng = 2 * half // span, rows // 128
    dma = pltpu.SemaphoreType.DMA
    return pl.pallas_call(
        functools.partial(finish_kernel, span),
        out_shape=(
            jax.ShapeDtypeStruct((block, 2 * half), F32),
            jax.ShapeDtypeStruct((rows // 2, depth), BF16),
            jax.ShapeDtypeStruct((rows // 2, depth), BF16),
            jax.ShapeDtypeStruct((1, 1), F32),
            jax.ShapeDtypeStruct((1, depth), F32),
            jax.ShapeDtypeStruct((1, depth), F32),
        ),
        in_specs=[ANY, ANY, VMEM],
        out_specs=(ANY, ANY, ANY, VMEM, VMEM, VMEM),
        scratch_shapes=[
            pltpu.VMEM((nf, span, block), F32),
            pltpu.VMEM((nf, block, span), F32),
            pltpu.VMEM((ng, 128, depth), BF16),
            dma((nf,)), dma((nf,)), dma((ng,)), dma((ng,)),
        ],
        compiler_params=pltpu.CompilerParams(vmem_limit_bytes=62 * 2**20),
        name="finish",
    )(fin, gh, tot)


def solution(mesh):
    n_tp, n_dp = mesh.shape["tp"], mesh.shape["dp"]

    def local_step(h_main, h_mtp, labels_main, labels_mtp, weight_main, weight_mtp, gain_final, gain_mtp, w_out):
        hm, ht = h_main[0], h_mtp[0]
        gm, gt = gain_final[None], gain_mtp[None]
        z, u_own, u_par, du_in, st, lpart = logits(n_tp, n_dp, hm, ht, gm, gt, labels_main, labels_mtp, weight_main, weight_mtp, w_out)
        fin, _, gh, _, tot = head_grad(n_tp, n_dp, hm, ht, gm, gt, u_own, u_par, z, w_out, st, du_in, lpart)
        grad_w, gh_m, gh_t, loss, gg_m, gg_t = finish(fin, gh, tot)
        return loss[0, 0], gh_m[None], gh_t[None], grad_w, gg_m[0], gg_t[0]

    row_spec = P("dp", None)
    return jax.shard_map(
        local_step,
        mesh=mesh,
        in_specs=(P("dp", None, None), P("dp", None, None), row_spec, row_spec, row_spec, row_spec, P(None), P(None), P(None, "tp")),
        out_specs=(P(), P("dp", None, None), P("dp", None, None), P("dp", "tp"), P(None), P(None)),
        check_vma=False,
    )
```

time: 510 us -> 247 us (0.48)
  Pallas kernels: 0 us -> 245 us
  waiting for transfers between devices: 213 us -> 0 us
  blocking collectives: 115 us -> 0 us
  matrix products: 107 us -> 0 us
  other arithmetic: 50.4 us -> 0 us
  between operations: 17 us -> 0.85 us
  local copies, waits for them, and re-layouts: 6.75 us -> 0 us
    pallas_call x0 -> x3, Pallas kernels: none -> 245 us  [the longest x1 166 us: head_grad(): pl.pallas_call(functools.partial(head_kernel, n_tp, n_dp, first, wide, ta...]
    reduce_scatter x1 -> x0, waiting for transfers between devices: 113 us -> none  [local_step(): grad_w = lax.psum_scatter(grad_w, 'dp', scatter_dimension=0, tiled=True)]
    dot_general x3 -> x0, matrix products: 107 us -> none  [the longest x1 35.7 us: local_step(): lax.dot_general(grad_z, w_out, (((1,), (1,)), ((), ())), preferred_elemen...]
    psum x1 -> x0, waiting for transfers between devices: 100 us -> none  [local_step(): lax.psum(grad_part.astype(jnp.float32), 'tp').reshape(2, rows, d_model)]
    psum x3 -> x0, blocking collectives: 79.9 us -> none  [the longest x1 29 us: local_step(): lax.psum(jnp.stack([jnp.sum(shifted, axis=-1), jnp.sum(jnp.where(is_targe...]
    pmax x1 -> x0, blocking collectives: 35.5 us -> none  [local_step(): row_max = lax.pmax(jnp.max(logits, axis=-1), 'tp')]
    convert_element_type x3 -> x0, other arithmetic: 27.9 us -> none  [the longest x1 18.3 us: local_step(): (row_w[:, None] * jnp.where(is_target, soft_probs - 1.0, soft_probs)).ast...]
    reduce_sum x6 -> x0, other arithmetic: 19.7 us -> none  [the longest x1 10.4 us: local_step(): jnp.sum(shifted, axis=-1)]
  transfers between devices with their start and end apart: 2 -> 0, of which waited for: 2 -> 0; matrix products, arithmetic and copies ran while one was open for 10% -> 0% of each run, Pallas kernels for 0% -> 0%
where the time goes in v2:
time: 247 us; the launch traced here: 246 us
  Pallas kernels  245 us (99%)
    pallas_call x1, Pallas kernels, head_grad(): pl.pallas_call(functools.partial(head_kernel, n_tp, n_dp, first, wide, ta...  166 us
    pallas_call x1, Pallas kernels, logits(): pl.pallas_call(functools.partial(logits_kernel, n_tp, n_dp, chunk, LEFT),...  69.7 us
    pallas_call x1, Pallas kernels, finish(): pl.pallas_call(functools.partial(finish_kernel, span), out_shape=(jax.Sha...  9.59 us

profile of v2, /device:TPU:1, one launch (start us, length us, event | category | flops | bytes accessed | tf_op | source)
XLA Modules:
  0.0 246.1 jit_solution(12361487367367992827)
XLA Ops:
  0.6 69.7 %logits.1 = (f32[1024,6400]{1,0:T(8,128)}, bf16[1024,2048]{1,0:T(8,128)(2,1)}, bf16[1024,2048]{1,0:T(8,128)(2,1)}, f32[1024,2048]{1,0:T(8,128)}, f32[2,8,1024]{2,1,0:T(8,128)}, /*index=5*/f32[8,128]{1,0:T(8,128)}) custom-call(bf16[512,2048]{1,0:T(8,128)(2,1)} %bitcast.9, bf16[512,2048]{1,0:T(8,128)(2,1)} %bitcast.11, f32[1,2048]{1,0:T(1,128)} %bitcast.15, ...), custom_call_target="tpu_custom_call" | custom-call | flops 26843545600 | bytes 26214400 | tf_op jit(solution)/shard_map/logits/pallas_call | solution.py:360
  70.4 165.9 %head_grad.1 = (f32[2,3200,256]{2,1,0:T(8,128)}, f32[1024,2048]{1,0:T(8,128)}, bf16[1024,2048]{1,0:T(8,128)(2,1)}, f32[1024,2048]{1,0:T(8,128)}, f32[4,2048]{1,0:T(4,128)}) custom-call(bf16[512,2048]{1,0:T(8,128)(2,1)} %bitcast.10, bf16[512,2048]{1,0:T(8,128)(2,1)} %bitcast.12, f32[1,2048]{1,0:T(1,128)} %bitcast.16, f32[1,2048]{1,0:T(1,128)} %bitcast.18, ...), custom_call_target="tpu_custom_call" | custom-call | flops 299999985664 | bytes 26214400 | tf_op jit(solution)/shard_map/head_grad/pallas_call | solution.py:854
  236.3 9.6 %finish.1 = (f32[256,6400]{1,0:T(8,128)}, bf16[512,2048]{1,0:T(8,128)(2,1)}, bf16[512,2048]{1,0:T(8,128)(2,1)}, f32[1,1]{1,0:T(1,128)}, f32[1,2048]{1,0:T(1,128)}, /*index=5*/f32[1,2048]{1,0:T(1,128)}) custom-call(f32[2,3200,256]{2,1,0:T(8,128)} %get-tuple-element.27.fin, bf16[1024,2048]{1,0:T(8,128)(2,1)} %get-tuple-element.28.gh, ...), custom_call_target="tpu_custom_call" | custom-call | tf_op jit(solution)/shard_map/finish/pallas_call | solution.py:948

commit v3 on v0

v3 whole, which is shorter than its diff:
```python
import functools

import jax
import jax.numpy as jnp
from jax import lax
from jax.experimental import pallas as pl
from jax.experimental.pallas import tpu as pltpu
from jax.sharding import PartitionSpec as P

NORM_EPS = 1e-6
MTP_LAMBDA = 0.3
F32, BF16 = jnp.float32, jnp.bfloat16
DMA = pltpu.SemaphoreType.DMA
TWO = DMA((2,))
ANY = pl.BlockSpec(memory_space=pl.ANY)
VMEM = pl.BlockSpec(memory_space=pltpu.VMEM)
VMEM_LIMIT = 67043328
WINDOW = 9
LANES, FEATS = 128, 256
RING = 4
WAYS = (1, -1)
BOTH = range(2)
NT = (((1,), (1,)), ((), ()))
CHUNK = 1280
LEFT = 4096
SLICE = 24
SPREAD = 2 * RING * RING * SLICE
FIRST, WIDE = 128, 384
TASK = 512
KINDS = "nnnnnsnsn"
DONE = (0, 5, 8, 16) + 5 * (20,)
ACTS = ("1a:f2,a1", "2t:L0", "3t:f3", "4t:C0", "2a:a2", "2d:L1,r00,u0", "3m:f4", "9t:a3,C1", "13t:L2,r01", "14t:C2", "3d:f5,r10,u1",
        "4m:r02", "18t:L3,a4", "19t:C3,r03", "4d:r11", "5m:r04", "5a:a5", "6m:r12,r05", "6a:a6", "7m:r13,r06", "7a:a7,r14,L4,g0")
TAIL = ("a8,C4,L5,r15,g1,C5,L6,C6,r16,r07,p70,q70,p71,q71,p80,q80", "p81,q81,r17,g2,r08,n,r18,z")


def ds(start, size, unit=8):
    return pl.ds(pl.multiple_of(start, unit), size)


def mod(p):
    return lax.rem(p + RING, RING)


def upto(n):
    return pl.ds(0, n)


def halves(n):
    return upto(n // 2), pl.ds(n // 2, n // 2)


def columns(row):
    return jnp.broadcast_to(row, (LANES, row.shape[1])).T


def near(src, dst, sem):
    return pltpu.make_async_copy(src, dst, sem)


def remote(src, dst, send, recv, to):
    return pltpu.make_async_remote_copy(src, dst, send, recv, device_id=to, device_id_type=pl.DeviceIdType.MESH)


def arrived(ref, sem):
    near(ref, ref, sem).wait()


def begin(copies):
    for c in copies:
        c.start()


def dot(a, b):
    return jnp.dot(a, b, preferred_element_type=F32)


def grad_logits(z, lse, rw, lab, col):
    lane = lax.broadcasted_iota(jnp.int32, z.shape, 1).astype(F32)
    p = jnp.exp(z - lse)
    return rw * jnp.where(lab - col == lane, p - 1.0, p)


class Torus:
    def __init__(self):
        self.tp, self.dp = lax.axis_index("tp"), lax.axis_index("dp")
        self.y, self.z = lax.rem(self.tp, RING), self.tp // RING
        self.x, self.core = self.dp // 2, lax.rem(self.dp, 2)
        self.mate = self.x + 1 - 2 * lax.rem(self.x, 2)
        self.far = RING - 1 - self.x
        self.opposite = RING - 1 - self.mate

    def side(self, swapped):
        return self.x // 2 if swapped else lax.rem((self.x + 1) // 2, 2)

    def chip(self, x, core=None):
        return {"tp": self.tp, "dp": 2 * x + (self.core if core is None else core)}

    def step(self, axis, d):
        y, z = (mod(self.y + d), self.z) if axis == 0 else (self.y, mod(self.z + d))
        return {"tp": z * RING + y, "dp": self.dp}

    def rings(self, s):
        ways = [functools.partial(self.step, a) for a in BOTH]
        return (self.y, ways[0], self.z, ways[1]) if s == 0 else (self.z, ways[1], self.y, ways[0])

    def others(self, axis):
        n, me = (lax.axis_size(axis), lax.axis_index(axis))
        return [{"tp": self.tp, "dp": self.dp, axis: lax.rem(me + d, n)} for d in range(1, n)]

    def greet(self):
        barrier = pltpu.get_barrier_semaphore()
        peers = self.others("tp") + self.others("dp")
        for peer in peers:
            pl.semaphore_signal(barrier, inc=1, device_id=peer, device_id_type=pl.DeviceIdType.MESH)
        return lambda: pl.semaphore_wait(barrier, len(peers))


class Exchange:
    def __init__(self, here, axis, src, land, send, recv):
        self.land, self.recv = land, recv
        me = lax.axis_index(axis)
        self.copies = lambda: [remote(src, land.at[me], send, recv, to) for to in here.others(axis)]
        self.rest = land.at[pl.ds(1, lax.axis_size(axis) - 1)]
        self.send, self.me = send, me

    def start(self, own):
        self.land[self.me] = own
        begin(self.copies())

    def blocks(self):
        arrived(self.rest, self.recv)
        return [self.land[i] for i in range(self.land.shape[0])]

    def drain(self):
        arrived(self.rest, self.send)


class Gather:
    def __init__(self, ref, rows, lanes, to, send, recv, own=None):
        self.ref, self.rows, self.to, self.send, self.recv = ref, rows, to, send, recv
        self.lanes = lanes
        self.own = ref.at[rows(0), lanes] if own is None else own
        self.size = rows(0).size

    def spread(self):
        dst = self.ref.at[self.rows(0), self.lanes]
        begin([remote(self.own, dst, self.send, self.recv.at[0], self.to(d)) for d in WAYS])

    def pass_on(self):
        arrived(self.ref.at[upto(2 * self.size), self.lanes], self.recv.at[0])
        n = self.lanes.size // 2
        for i, d in enumerate(WAYS):
            part = self.ref.at[self.rows(-d), pl.ds(self.lanes.start + i * n, n)]
            remote(part, part, self.send, self.recv.at[1], self.to(d)).start()

    def end(self):
        arrived(self.ref.at[upto(self.size), self.lanes], self.recv.at[1])


class Scatter:
    def __init__(self, src, rows, to, from_a, from_b, send, recv):
        self.src, self.rows, self.to, self.a, self.b, self.send, self.recv = src, rows, to, from_a, from_b, send, recv
        self.lanes = halves(src.shape[-1])

    def start(self):
        for i, d in enumerate(WAYS):
            remote(self.src.at[self.rows(2), self.lanes[i]], self.a.at[i], self.send, self.recv.at[0], self.to(d)).start()

    def rest(self):
        for i, d in enumerate(WAYS):
            other = self.lanes[1 - i]
            remote(self.src.at[self.rows(d), other], self.b.at[i, :, other], self.send, self.recv.at[1], self.to(d)).start()

    def middle(self, own):
        arrived(self.a, self.recv.at[0])
        for i, d in enumerate(WAYS):
            self.a[i] += own(i, d)
            remote(self.a.at[i], self.b.at[i, :, self.lanes[i]], self.send, self.recv.at[1], self.to(d)).start()

    def end(self):
        arrived(self.b, self.recv.at[1])


def slices(here, s):
    p1, _, p2, _ = here.rings(s)
    base = s * (SPREAD // 2)
    return (lambda o: ds(base + (p2 * RING + mod(p1 + o)) * SLICE, SLICE)), (lambda o: ds(base + mod(p2 + o) * RING * SLICE, RING * SLICE))


def plane_gather(here, ref, s, send, recv):
    _, to1, _, to2 = here.rings(s)
    one, many = slices(here, s)
    depth = ref.shape[-1]
    a = Gather(ref, one, upto(depth), to1, send.at[s], recv.at[s, 0])
    b, c = [Gather(ref, many, lanes, to2, send.at[s], recv.at[s, i + 1]) for i, lanes in enumerate(halves(depth))]

    def turn():
        a.end()
        b.spread()

    def end():
        b.end()
        c.end()

    def drain():
        arrived(ref.at[upto(3 * (RING + 1) * SLICE), :], send.at[s])

    return [a.spread, a.pass_on, turn, c.spread, b.pass_on, c.pass_on, end, drain]


def logits_kernel(hm, ht, gain_m, gain_t, lab_m, lab_t, wt_m, wt_t, w, z, u_out, up_out, far_u, du_out, st, lpart,
                  h_v, u_v, uf_v, got_v, w_v, z_v, e_v, x_v, m_v, s_v, t_v, lab_v, send_v, land, wsend, wland, pack,
                  sem_h, sem_u, sem_w, sem_z, sem_d, sem_k, es, er, ps, pr, gs, gr, xs, xr):
    seq, depth = hm.shape
    rows, vocab = z.shape
    steps = vocab // CHUNK
    here = Torus()
    mate, far = here.chip(here.mate), here.chip(here.far)

    def w_copy(i, slot):
        return near(w.at[:, ds(i * CHUNK, CHUNK, LANES)], w_v.at[slot], sem_w.at[slot])

    def z_copy(i, slot):
        return near(z_v.at[slot], z.at[:, ds(i * CHUNK, CHUNK, LANES)], sem_z.at[slot])

    loads = [near(src, h_v.at[pl.ds(i * seq, seq), :], sem_h.at[i]) for i, src in enumerate((hm, ht))]
    begin(loads + [w_copy(0, 0)])
    met = here.greet()
    m_v[:] = jnp.full_like(m_v, -jnp.inf)
    s_v[:] = jnp.zeros_like(s_v)
    t_v[:] = jnp.zeros_like(t_v)
    lab = jnp.concatenate([lab_m[:], lab_t[:]], axis=1).astype(F32) - (here.tp * vocab).astype(F32)
    lab_v[:] = columns(lab)
    top_row = lax.broadcasted_iota(jnp.int32, wsend.shape, 0) == 0
    wsend[:] = jnp.where(top_row, jnp.sum(wt_m[:]), jnp.sum(wt_t[:]))

    for half, gain in enumerate((gain_m, gain_t)):
        loads[half].wait()
        g = gain[:]

        @pl.loop(0, seq // LANES)
        def _(i):
            r = ds(half * seq + i * LANES, LANES)
            x = h_v[r, :].astype(F32)
            inv = lax.rsqrt(jnp.mean(x * x, axis=-1, keepdims=True) + NORM_EPS)
            u = (x * inv * g).astype(BF16)
            u_v[r, :] = u
            uf_v[r, :] = u.astype(F32)

    u_copy = near(u_v, u_out, sem_u)
    u_copy.start()
    with jax.named_scope("meet"):
        met()

    weights = Exchange(here, "dp", wsend, wland, es.at[0], er.at[0])
    weights.start(wsend[:])
    rest = pl.ds(SPREAD, rows - SPREAD)
    parts = [slices(here, s)[0](0) for s in BOTH] + [rest]

    def fetched(k, i):
        return remote(uf_v.at[parts[i], :], (got_v, far_u)[k].at[parts[i], :], xs.at[k, i], xr.at[k, i], (mate, far)[k])

    begin([fetched(k, i) for i in range(3) for k in BOTH])
    spread = [plane_gather(here, got_v, s, gs, gr) for s in BOTH]
    lane = lax.broadcasted_iota(jnp.int32, (rows, LANES), 1).astype(F32)

    @pl.loop(0, steps)
    def _(i):
        slot = lax.rem(i, 2)
        w_copy(i, slot).wait()

        @pl.when(i + 1 < steps)
        def _():
            w_copy(i + 1, 1 - slot).start()

        @pl.when(i >= 2)
        def _():
            z_copy(i - 2, slot).wait()

        m, s, t = m_v[:], s_v[:], t_v[:]
        rel = lab_v[:] - (i * CHUNK).astype(F32)
        for n in range(0, CHUNK, FEATS):
            for which, at in enumerate((0, 3 * FEATS)):
                for stage in range(3):
                    if n == at:
                        @pl.when(i == stage + 1)
                        def _():
                            if stage == 0:
                                arrived(got_v.at[parts[which], :], xr.at[0, which])
                            spread[which][stage]()
            zz = dot(u_v[:], w_v[slot, :, n:n + FEATS])
            z_v[slot, :, n:n + FEATS] = zz
            za, zb = zz[:, :LANES], zz[:, LANES:]
            new = jnp.maximum(m, jnp.maximum(za, zb))
            s = s * jnp.exp(m - new) + (jnp.exp(za - new) + jnp.exp(zb - new))
            t = jnp.where(rel == lane + n, za, t)
            t = jnp.where(rel == lane + (n + LANES), zb, t)
            m = new
        m_v[:], s_v[:], t_v[:] = m, s, t
        z_copy(i, slot).start()

    mt = m_v[:].T
    top = jnp.max(mt, axis=0, keepdims=True)
    total = jnp.sum(s_v[:].T * jnp.exp(mt - top), axis=0, keepdims=True)
    hit = jnp.sum(t_v[:].T, axis=0, keepdims=True)
    send_v[:] = jnp.where(lax.broadcasted_iota(jnp.int32, send_v.shape, 0) == 0, top + jnp.log(total), hit)
    stats = Exchange(here, "tp", send_v, land, es.at[1], er.at[1])
    stats.start(send_v[:])
    for stage in (3, 4):
        for which in BOTH:
            spread[which][stage]()
    sums = functools.reduce(jnp.add, weights.blocks())
    rw = jnp.concatenate([wt_m[:] * (1.0 / sums[0:1, 0:1]), wt_t[:] * (MTP_LAMBDA / sums[1:2, 0:1])], axis=1)
    with jax.named_scope("statwait"):
        blocks = stats.blocks()
    top = functools.reduce(jnp.maximum, blocks)
    lse = (top + jnp.log(functools.reduce(jnp.add, [jnp.exp(b - top) for b in blocks])))[0:1, :]
    hit = functools.reduce(jnp.add, blocks)[1:2, :]
    lpart[:] = jnp.broadcast_to(jnp.sum(rw * (lse - hit)), lpart.shape)
    row = lax.broadcasted_iota(jnp.int32, st.shape[1:], 0)
    st[1] = jnp.where(row == 0, lse, jnp.where(row == 1, rw, lab))
    pack[:] = st[1]
    swaps = [remote(pack, st.at[2 * k], ps.at[k], pr.at[k], to) for k, to in enumerate((mate, far))]
    begin(swaps)
    m_v[:] = columns(lse)
    s_v[:] = columns(rw)
    skip = LEFT - (steps - 2) * CHUNK
    at = 0
    for step, start in ((steps - 1, 0), (steps - 2, skip)):
        for c in range(start, CHUNK, LANES):
            e_v[:, at:at + LANES] = grad_logits(
                z_v[step % 2, :, c:c + LANES], m_v[:], s_v[:], lab_v[:], float(step * CHUNK + c)).astype(BF16)
            at += LANES

    def e_dot(r, cols):
        return (lax.dot_general(e_v[r, :CHUNK], w_v[(steps - 1) % 2, cols, :], NT, preferred_element_type=F32)
                + lax.dot_general(e_v[r, CHUNK:], w_v[(steps - 2) % 2, cols, skip:], NT, preferred_element_type=F32))

    for i in BOTH:
        for k in BOTH:
            fetched(k, i).wait_send()
    saves = []
    for dst, r in ((uf_v, slice(0, SPREAD)), (x_v, slice(SPREAD, rows))):
        for n in range(0, depth, TASK):
            dst[:r.stop - r.start, n:n + TASK] = e_dot(r, slice(n, n + TASK))
            src = dst.at[upto(r.stop - r.start), pl.ds(n, TASK)]
            saves.append(near(src, du_out.at[pl.ds(r.start, r.stop - r.start), pl.ds(n, TASK)], sem_d.at[len(saves)]))
            saves[-1].start()
            if len(saves) in (2, 3):
                spread[len(saves) - 2][5]()
    u_copy.wait()
    waits = [spread[0][6], spread[1][6], lambda: arrived(got_v.at[rest, :], xr.at[0, 2])]
    for i, wait in enumerate(waits):
        start = i * (SPREAD // 2)
        r = pl.ds(start, min(SPREAD // 2, rows - start))
        with jax.named_scope("land"):
            wait()

        @pl.loop(start // LANES, (start + r.size) // LANES)
        def _(j):
            part = ds(j * LANES, LANES)
            u_v[part, :] = got_v[part, :].astype(BF16)

        saves.append(near(u_v.at[r, :], up_out.at[r, :], sem_k.at[i]))
        saves[-1].start()
    for c in swaps:
        c.wait()
    for i in range(3):
        arrived(far_u.at[parts[i], :], xr.at[1, i])
    weights.drain()
    stats.drain()
    for k in BOTH:
        spread[k][7]()
        fetched(k, 2).wait_send()
        z_copy(steps - 2 + k, (steps + k) % 2).wait()
    for c in saves:
        c.wait()


def logits(hm, ht, gain_m, gain_t, lab_m, lab_t, wt_m, wt_t, w):
    seq, depth = hm.shape
    rows, vocab = 2 * seq, w.shape[1]
    n_tp, n_dp = lax.axis_size("tp"), lax.axis_size("dp")
    shape = jax.ShapeDtypeStruct
    stat = pltpu.VMEM((rows, LANES), F32)
    return pl.pallas_call(
        logits_kernel,
        out_shape=(shape((rows, vocab), F32), shape((rows, depth), BF16), shape((rows, depth), BF16), shape((rows, depth), F32),
                   shape((rows, depth), F32), shape((3, 8, rows), F32), shape((8, LANES), F32)),
        in_specs=[ANY, ANY] + [VMEM] * 6 + [ANY],
        out_specs=(ANY,) * 5 + (VMEM, VMEM),
        scratch_shapes=[
            pltpu.VMEM((rows, depth), BF16), pltpu.VMEM((rows, depth), BF16), pltpu.VMEM((rows, depth), F32), pltpu.VMEM((rows, depth), F32),
            pltpu.VMEM((2, depth, CHUNK), BF16), pltpu.VMEM((2, rows, CHUNK), F32), pltpu.VMEM((rows, vocab - LEFT), BF16),
            pltpu.VMEM((rows - SPREAD, depth), F32), stat, stat, stat, stat,
            pltpu.VMEM((2, rows), F32), pltpu.VMEM((n_tp, 2, rows), F32), pltpu.VMEM((8, LANES), F32), pltpu.VMEM((n_dp, 8, LANES), F32),
            pltpu.VMEM((8, rows), F32),
            TWO, DMA, TWO, TWO, DMA((2 * depth // TASK,)), DMA((3,)), TWO, TWO, TWO, TWO,
            TWO, DMA((2, 3, 2)), *[DMA((2, 3))] * 2,
        ],
        compiler_params=pltpu.CompilerParams(vmem_limit_bytes=VMEM_LIMIT, collective_id=0, has_side_effects=True),
        name="logits",
    )(hm, ht, gain_m, gain_t, lab_m, lab_t, wt_m, wt_t, w)


def chunk_table():
    out, at, used = [], 0, [0, 0]
    for i, kind in enumerate(KINDS):
        width, swapped = (WIDE if i else FIRST), int(kind == "s")
        out.append((at, width, swapped, used[swapped]))
        at, used[swapped] = at + width, used[swapped] + width
    return out, used


def column(here, used, swapped, other, offset):
    base = [2 * used[0] * s + abs(here.side(s) - other) * used[s] for s in BOTH]
    return jnp.where(swapped == 1, base[1], base[0]) + offset


def pick(values, k):
    if isinstance(k, int):
        return values[k]
    return functools.reduce(lambda out, i: jnp.where(k == i, values[i], out), range(1, len(values)), jnp.int32(values[0]))


def head_kernel(hm, ht, gain_m, gain_t, u_own, u_par, far_in, z, w, st, du_in, lpart,
                fin, gh, ghb, du, far_u, one, tot, u_v, w_v, z_v, et_v, g_v, own_v, sum_v, one_v, acc_v,
                lse_v, rw_v, lab_v, ra_v, rl_v, rb_v, rm_v, ra2_v, rb2_v, rh_v, gg_v, gland, tland, tsend,
                sem_u, sem_w, sem_z, sem_a, sem_o, sem_1, d_send, d_recv, b_send, b_recv, f_send, f_recv,
                gs, gr, ss, sr, sem_l, sem_x, es, er):
    del far_in
    rows, depth = u_own.shape
    seq = rows // 2
    here = Torus()
    x, core = here.x, here.core
    met = here.greet()
    table, used = chunk_table()
    starts, _, swaps, offsets = (list(t) for t in zip(*table))
    last = len(table) - 1

    def span(k):
        return upto(FIRST) if isinstance(k, int) and k == 0 else ds(FIRST + (k - 1) * WIDE, WIDE, LANES)

    def chips(k):
        s = pick(swaps, k) == 1
        return jnp.where(s, here.far, here.mate), jnp.where(s, here.mate, here.far)

    def block(i):
        return ds((2 * lax.rem(i, RING) + jnp.where(i < RING, 1 - core, core)) * FEATS, FEATS, FEATS)

    def feats(i):
        return pl.ds(i * FEATS, FEATS)

    def w_copies(col, width, slot):
        return [near(w.at[block(i), ds(col, width, LANES)], w_v.at[slot, feats(i), upto(width)], sem_w.at[slot]) for i in range(2 * RING)]

    def u_copies(k):
        src, r = ((u_par, upto(rows)), (u_own, pl.ds(rows, rows)))[k]
        return [near(src.at[:, block(i)], u_v.at[r, feats(i)], sem_u.at[k]) for i in range(2 * RING)]

    def u_wait(k):
        arrived(u_v.at[upto(rows), :], sem_u.at[k])

    def fetch(k, slot):
        width = span(k).size
        col = column(here, used, pick(swaps, k), 0, pick(offsets, k))
        begin(w_copies(col, width, slot) + [near(z.at[:, ds(col, width, LANES)], z_v.at[slot, :, upto(width)], sem_z.at[slot])])

    per = LEFT // TASK

    def piece(t):
        return t < 2 * per, t // per, lax.rem(t, per)

    def acc_copies(h, back):
        refs = [(acc_v.at[:, feats(i)], (du if back else du_in).at[ds(h * seq, seq), block(i)]) for i in range(2 * RING)]
        return [near(*(p if back else p[::-1]), sem_a) for p in refs]

    def task_fetch(t, slot):
        of_du, h, i = piece(t)

        @pl.when(of_du)
        def _():
            begin(w_copies(i * TASK, TASK, slot))
            near(z.at[ds(h * seq, seq), ds(i * TASK, TASK, LANES)], z_v.at[slot, upto(seq), :], sem_z.at[slot]).start()

        @pl.when(~of_du)
        def _():
            begin([near(far_u.at[:, block(2 * i + j)], z_v.at[slot, :, feats(j)], sem_z.at[slot]) for j in BOTH])

    def task(t, slot):
        of_du, h, i = piece(t)

        @pl.when(~of_du)
        def _():
            arrived(z_v.at[slot], sem_z.at[slot])
            u_v[pl.ds(2 * rows, rows), ds(i * TASK, TASK, LANES)] = z_v[slot].astype(BF16)

        @pl.when(of_du)
        def _():
            arrived(w_v.at[slot], sem_w.at[slot])
            arrived(z_v.at[slot, upto(seq), :], sem_z.at[slot])

            @pl.when(i == 0)
            def _():
                arrived(acc_v, sem_a)

            r = ds(rows + h * seq, seq)
            col = (i * TASK).astype(F32)
            for g in range(0, TASK, LANES):
                cols = slice(g, g + LANES)
                et_v[:, cols] = grad_logits(z_v[slot, :seq, cols], lse_v[r, :], rw_v[r, :], lab_v[r, :], col + g).astype(BF16)
            for m in range(0, depth, TASK):
                cols = slice(m, m + TASK)
                acc_v[:, cols] += lax.dot_general(et_v[:, :TASK], w_v[slot, cols, :], NT, preferred_element_type=F32)

            @pl.when(i == per - 1)
            def _():
                acc_v[:] = acc_v[:].astype(BF16).astype(F32)
                begin(acc_copies(h, True))
                arrived(acc_v, sem_a)

            @pl.when((i == per - 1) & (h == 0))
            def _():
                begin(acc_copies(1, False))

    def d_copy(k, part):
        lanes, width = pl.ds(part * TASK, TASK), span(k).size
        return remote(g_v.at[upto(width), lanes], sum_v.at[span(k), lanes], d_send, d_recv.at[k], here.chip(x, 1 - core))

    def b_copy(k, which):
        to = chips(k)[1]
        block_of = ds(jnp.where(which == 0, here.opposite, to) * FEATS, FEATS, FEATS)
        return remote(sum_v.at[span(k), block_of], one.at[which, span(k), :], b_send, b_recv.at[k, which], here.chip(to))

    def f_copy(k):
        mate = chips(k)[0]
        return remote(sum_v.at[span(k), ds(mate * FEATS, FEATS, FEATS)], fin.at[1, span(k), :], f_send, f_recv, here.chip(mate))

    def o_copy(k):
        return near(sum_v.at[span(k), ds(x * FEATS, FEATS, FEATS)], fin.at[0, span(k), :], sem_o)

    def make(k, slot, early=lambda: None, late=lambda: None, middle=lambda: None):
        width = span(k).size
        swapped = pick(swaps, k)
        col = column(here, used, swapped, 0, pick(offsets, k)).astype(F32)
        arrived(w_v.at[slot, :, upto(width)], sem_w.at[slot])
        arrived(z_v.at[slot, :, upto(width)], sem_z.at[slot])
        early()

        def put(zz, r, c, at):
            e = grad_logits(zz, lse_v[r, :], rw_v[r, :], lab_v[r, :], col + c)
            et_v[c:c + LANES, ds(at, rows, rows)] = e.T.astype(BF16)

        for c in range(0, width, LANES):
            put(z_v[slot, :, c:c + LANES], pl.ds(rows, rows), c, rows * (1 - swapped))
        late()
        other = ds(2 * rows * swapped, rows, rows)
        for n in range(0, width, FEATS):
            step = min(width - n, FEATS)
            zz = dot(u_v[other, :], w_v[slot, :, n:n + step])
            for c in range(0, step, LANES):
                put(zz[:, c:c + LANES], other, n + c, rows * swapped)
        middle()
        both = ds(rows * swapped, 2 * rows, rows)
        et = et_v[upto(width), :]
        for part in BOTH:
            lanes = pl.ds(part * TASK, TASK)
            g_v[upto(width), lanes] = dot(et, u_v[both, lanes])
            d_copy(k, part).start()
        own_v[upto(width), :] = dot(et, u_v[both, pl.ds(2 * TASK, 2 * TASK)])

    def add(k):
        arrived(sum_v.at[span(k), :], d_recv.at[k])
        sum_v[span(k), :] += own_v[upto(span(k).size), :]
        begin([b_copy(k, which) for which in BOTH])

    def landing(k, which):
        return near(one.at[which, span(k), :], one_v.at[which, upto(span(k).size), :], sem_1.at[which])

    def land(k, which):
        with jax.named_scope("bwait"):
            arrived(one.at[which, span(k), :], b_recv.at[k, which])
        landing(k, which).start()

    def close(k, which):
        landing(k, which).wait()
        chip = jnp.where(which == 0, chips(k)[0], x)
        sum_v[span(k), ds(chip * FEATS, FEATS, FEATS)] += one_v[which, upto(span(k).size), :]
        (o_copy if which else f_copy)(k).start()

    def ring(h, s):
        q = 2 * h + s
        p1, to1, p2, to2 = here.rings(s)
        big, small = seq // 2 // RING, seq // 2 // RING // RING
        base = h * seq + s * (seq // 2)
        one_of = lambda o: ds(base + mod(p1 + o) * big, big)
        two_of = lambda o: ds(base + p1 * big + mod(p2 + o) * small, small)
        sub = lambda o: ds(mod(p2 + o) * small, small)
        every = upto(depth)
        first = Scatter(du, one_of, to1, ra_v.at[q], rb_v.at[q], ss.at[q], sr.at[q, 0])
        second = Scatter(rm_v.at[q], sub, to2, ra2_v.at[q], rb2_v.at[q], ss.at[q], sr.at[q, 1])
        down = Gather(gh, two_of, every, to2, ss.at[q], sr.at[q, 2], rm_v.at[q, sub(0), :])
        up = Gather(gh, one_of, every, to1, ss.at[q], sr.at[q, 3])
        lanes = halves(depth)
        h_rows = ds(s * (seq // 2) + p1 * big + p2 * small, small)
        loads = lambda: [near(du.at[one_of(WAYS[i]), lanes[i]], rl_v.at[s, i], sem_l.at[s, i]) for i in BOTH] + [
            near(du.at[one_of(0), :], rm_v.at[q], sem_l.at[s, 2]), near((hm, ht)[h].at[h_rows, :], rh_v.at[q], sem_l.at[s, 3])]
        keep = lambda: near(rm_v.at[q, sub(0), :], gh.at[two_of(0), :], sem_x.at[q])
        return q, sub, lanes, first, second, down, up, loads, keep

    def event(h, stage):
        for s in BOTH:
            q, sub, lanes, first, second, down, up, loads, keep = ring(h, s)
            if stage == 0:
                first.start()
                begin(loads())
            if stage == 1:
                for c in loads():
                    c.wait()
                first.middle(lambda i, d: rl_v[s, i])
            if stage == 2:
                first.end()
                rm_v[q] += rb_v[q, 0] + rb_v[q, 1]
                second.start()
                second.rest()
            if stage == 3:
                second.middle(lambda i, d: rm_v[q, sub(d), lanes[i]])
            if stage == 4:
                second.end()
                gu = rm_v[q, sub(0), :] + (rb2_v[q, 0] + rb2_v[q, 1])
                xr = rh_v[q].astype(F32)
                inv = lax.rsqrt(jnp.mean(xr * xr, axis=-1, keepdims=True) + NORM_EPS)
                normed = xr * inv
                gn = gu * (gain_m, gain_t)[h][:]
                gx = inv * (gn - normed * jnp.mean(gn * normed, axis=-1, keepdims=True))
                rm_v[q, sub(0), :] = gx.astype(BF16).astype(F32)
                part = jnp.sum(gu * normed, axis=0, keepdims=True)
                gg_v[pl.ds(h, 1), :] = part if s == 0 else gg_v[pl.ds(h, 1), :] + part
                keep().start()
                down.spread()
            if stage == 5:
                down.pass_on()
            if stage == 6:
                keep().wait()
                down.end()
                up.spread()
            if stage == 7:
                up.pass_on()
            if stage == 8:
                up.end()

    def rest(h):
        for s in BOTH:
            ring(h, s)[3].rest()

    plane = Exchange(here, "tp", gg_v, gland, es.at[0], er.at[0])
    line = Exchange(here, "dp", tsend, tland, es.at[1], er.at[1])

    def sums(stage):
        if stage == 0:
            plane.start(gg_v[:])
        if stage == 1:
            total = functools.reduce(jnp.add, plane.blocks())
            tsend[:] = jnp.concatenate([total, jnp.broadcast_to(lpart[0:1, 0:1], total.shape)])
            line.start(tsend[:])
        if stage == 2:
            tot[:] = functools.reduce(jnp.add, line.blocks())

    def narrow():
        r = upto(seq)
        c = near(gh.at[r, :], acc_v, sem_a)
        c.start()
        c.wait()
        u_v[r, :] = acc_v[:].astype(BF16)
        near(u_v.at[r, :], ghb, sem_a).start()

    far_steps = [plane_gather(here, far_u, s, gs, gr) for s in BOTH]

    def far_event(stage):
        for s in BOTH:
            for i in ((stage - 1,), (2, 3), (4, 5), (6,))[max(stage - 2, 0)]:
                far_steps[s][i]()

    def drain():
        rows_sent = 6 * (seq // 2 // RING + seq // 2 // RING // RING)
        for q in range(4):
            arrived(du.at[upto(rows_sent), :], ss.at[q])
        for s in BOTH:
            far_steps[s][7]()
        plane.drain()
        line.drain()
        arrived(sum_v.at[:, upto(2 * FEATS)], b_send)
        arrived(g_v, d_send)

    def both(act):
        return lambda k: [act(k, which) for which in BOTH]

    verbs = {"r": event, "u": rest, "g": sums, "n": narrow, "f": far_event, "a": add, "L": both(land), "C": both(close), "p": land, "q": close, "z": drain}

    def run(text):
        for word in text.split(","):
            with jax.named_scope(word):
                verbs[word[0]](*(int(c) for c in word[1:]))

    def at_point(k, point):
        for at, text in (a.split(":") for a in ACTS):
            if at[-1] == point:
                @pl.when(k == int(at[:-1]))
                def _():
                    run(text)

    fetch(0, 0)
    begin(u_copies(0))

    def spread_stats(k):
        for i, ref in enumerate((lse_v, rw_v, lab_v)):
            ref[pl.ds(k * rows, rows), :] = columns(st[k, i:i + 1, :])

    spread_stats(1)

    def more_loads():
        begin(u_copies(1))
        fetch(1, 1)
        begin(acc_copies(0, False))

    def before_other():
        spread_stats(0)
        u_wait(0)

    def before_sends():
        spread_stats(2)
        u_wait(1)
        with jax.named_scope("meet"):
            met()
        far_event(1)

    with jax.named_scope("make0"):
        make(0, 0, more_loads, before_other, before_sends)
    add(0)

    @pl.loop(1, last + 1)
    def _(k):
        lo, hi = pick(DONE[:1] + DONE[:-1], k), pick(DONE, k)
        slot = lax.rem(k + lo, 2)

        def more(t):
            @pl.when(t < hi)
            def _():
                task_fetch(t, lax.rem(k + 1 + t, 2))

            @pl.when((t == hi) & (k < last))
            def _():
                fetch(k + 1, lax.rem(k + 1 + t, 2))

        more(lo)

        def middle():
            at_point(k, "m")

            @pl.when(k == 1)
            def _():
                arrived(g_v.at[upto(FIRST), :], d_send)

            @pl.when(k > 1)
            def _():
                arrived(g_v, d_send)

        with jax.named_scope("make"):
            make(k, slot, middle=middle)

        at_point(k, "a")

        @pl.loop(lo, hi)
        def _(t):
            at_point(t, "t")
            more(t + 1)
            with jax.named_scope("task"):
                task(t, lax.rem(k + 1 + t, 2))

        at_point(k, "d")

    for text in TAIL:
        run(text)
    with jax.named_scope("tail"):
        arrived(fin.at[1], f_send)
        arrived(fin.at[1], f_recv)
        arrived(fin.at[0], sem_o)
        arrived(ghb, sem_a)


def head_grad(hm, ht, gain_m, gain_t, u_own, u_par, far_u, z, w, st, du_in, lpart):
    rows, depth = u_own.shape
    seq = rows // 2
    half = z.shape[1] // 2
    n_tp, n_dp, n = lax.axis_size("tp"), lax.axis_size("dp"), len(KINDS)
    big, small = seq // 2 // RING, seq // 2 // RING // RING
    shape = jax.ShapeDtypeStruct
    stat = pltpu.VMEM((3 * rows, LANES), F32)
    return pl.pallas_call(
        head_kernel,
        out_shape=(shape((2, half, FEATS), F32), shape((rows, depth), F32), shape((seq, depth), BF16), shape((rows, depth), F32),
                   shape((rows, depth), F32), shape((2, half, FEATS), F32), shape((4, depth), F32)),
        in_specs=[ANY, ANY, VMEM, VMEM] + [ANY] * 5 + [VMEM, ANY, VMEM],
        out_specs=(ANY,) * 6 + (VMEM,),
        scratch_shapes=[
            pltpu.VMEM((3 * rows, depth), BF16), pltpu.VMEM((2, depth, TASK), BF16), pltpu.VMEM((2, rows, TASK), F32),
            pltpu.VMEM((TASK, 2 * rows), BF16), pltpu.VMEM((WIDE, 2 * TASK), F32), pltpu.VMEM((WIDE, 2 * TASK), F32),
            pltpu.VMEM((half, 2 * TASK), F32), pltpu.VMEM((2, WIDE, FEATS), F32), pltpu.VMEM((seq, depth), F32),
            stat, stat, stat,
            pltpu.VMEM((4, 2, big, depth // 2), F32), pltpu.VMEM((2, 2, big, depth // 2), F32), pltpu.VMEM((4, 2, big, depth), F32),
            pltpu.VMEM((4, big, depth), F32), pltpu.VMEM((4, 2, small, depth // 2), F32), pltpu.VMEM((4, 2, small, depth), F32),
            pltpu.VMEM((4, small, depth), BF16),
            pltpu.VMEM((2, depth), F32), pltpu.VMEM((n_tp, 2, depth), F32), pltpu.VMEM((n_dp, 4, depth), F32), pltpu.VMEM((4, depth), F32),
            TWO, TWO, TWO, DMA, DMA, TWO, DMA, DMA((n,)), DMA, DMA((n, 2)), DMA, DMA,
            TWO, DMA((2, 3, 2)), DMA((4,)), DMA((4, 4, 2)), DMA((2, 4)), DMA((4,)), TWO, TWO,
        ],
        input_output_aliases={6: 4},
        compiler_params=pltpu.CompilerParams(vmem_limit_bytes=VMEM_LIMIT, collective_id=1, has_side_effects=True),
        name="head_grad",
    )(hm, ht, gain_m, gain_t, u_own, u_par, far_u, z, w, st, du_in, lpart)


def finish_kernel(fin, gh, ghb, tot, out, gm, gt, loss, ggm, ggt, f_v, o_v, g_v, m_v, t_v, sem_f, sem_o, sem_g):
    seq = gm.shape[0]
    table, used = chunk_table()
    jobs = [(k, *t) for t in table for k in BOTH]
    here = Torus()

    def f_in(i):
        k, at, width, _, _ = jobs[i]
        return near(fin.at[k, pl.ds(at, width), :], f_v.at[k, pl.ds(at, width), :], sem_f.at[i])

    def f_out(i):
        k, at, width, swapped, offset = jobs[i]
        return near(o_v.at[k, :, pl.ds(at, width)], out.at[:, ds(column(here, used, swapped, k, offset), width, LANES)], sem_o.at[i])

    g_in, m_in = near(gh.at[pl.ds(seq, seq), :], g_v, sem_g.at[0]), near(ghb, m_v, sem_g.at[1])
    begin([f_in(i) for i in range(WINDOW)])
    ggm[:], ggt[:], loss[:] = tot[0:1, :], tot[1:2, :], tot[2:3, 0:1]
    outs = [f_out(i) for i in range(len(jobs))] + [near(t_v, gt, sem_g.at[0]), near(m_v, gm, sem_g.at[1])]
    for i, (k, at, width, _, _) in enumerate(jobs):
        begin([f_in(i + WINDOW)] if i + WINDOW < len(jobs) else [(m_in, g_in)[i % 2]] if i + 2 >= len(jobs) else [])
        f_in(i).wait()
        o_v[k, :, pl.ds(at, width)] = f_v[k, pl.ds(at, width), :].T
        outs[i].start()
    m_in.wait()
    outs[-1].start()
    g_in.wait()
    t_v[:] = g_v[:].astype(BF16)
    outs[-2].start()
    for c in outs:
        c.wait()


def finish(fin, gh, ghb, tot):
    _, half, block = fin.shape
    seq, depth = ghb.shape
    shape, row, jobs = jax.ShapeDtypeStruct, jax.ShapeDtypeStruct((1, depth), F32), DMA((2 * len(KINDS),))
    rows = pltpu.VMEM((seq, depth), BF16)
    return pl.pallas_call(
        finish_kernel,
        out_shape=(shape((block, 2 * half), F32), shape((seq, depth), BF16), shape((seq, depth), BF16), shape((1, 1), F32), row, row),
        in_specs=[ANY, ANY, ANY, VMEM],
        out_specs=(ANY, ANY, ANY, VMEM, VMEM, VMEM),
        scratch_shapes=[pltpu.VMEM((2, half, block), F32), pltpu.VMEM((2, block, half), F32), pltpu.VMEM((seq, depth), F32), rows, rows,
                        jobs, jobs, TWO],
        compiler_params=pltpu.CompilerParams(vmem_limit_bytes=VMEM_LIMIT),
        name="finish",
    )(fin, gh, ghb, tot)


def solution(mesh):
    def local_step(h_main, h_mtp, labels_main, labels_mtp, weight_main, weight_mtp, gain_final, gain_mtp, w_out):
        hm, ht, gm, gt = h_main[0], h_mtp[0], gain_final[None], gain_mtp[None]
        z, u_own, u_par, far_u, du_in, st, lpart = logits(hm, ht, gm, gt, labels_main, labels_mtp, weight_main, weight_mtp, w_out)
        fin, gh, ghb, _, _, _, tot = head_grad(hm, ht, gm, gt, u_own, u_par, far_u, z, w_out, st, du_in, lpart)
        grad_w, gh_m, gh_t, loss, gg_m, gg_t = finish(fin, gh, ghb, tot)
        return loss[0, 0], gh_m[None], gh_t[None], grad_w, gg_m[0], gg_t[0]

    wide, row = P("dp", None, None), P("dp", None)
    return jax.shard_map(
        local_step,
        mesh=mesh,
        in_specs=(wide, wide, row, row, row, row, P(None), P(None), P(None, "tp")),
        out_specs=(P(), wide, wide, P("dp", "tp"), P(None), P(None)),
        check_vma=False,
    )
```

time: 510 us -> 240 us (0.47)
  Pallas kernels: 0 us -> 238 us
  waiting for transfers between devices: 213 us -> 0 us
  blocking collectives: 115 us -> 0 us
  matrix products: 107 us -> 0 us
  other arithmetic: 50.4 us -> 0 us
  between operations: 17 us -> 0.83 us
  local copies, waits for them, and re-layouts: 6.75 us -> 0 us
    pallas_call x0 -> x3, Pallas kernels: none -> 238 us  [the longest x1 160 us: head_grad(): pl.pallas_call(head_kernel, out_shape=(shape((2, half, FEATS), F32), shap...]
    reduce_scatter x1 -> x0, waiting for transfers between devices: 113 us -> none  [local_step(): grad_w = lax.psum_scatter(grad_w, 'dp', scatter_dimension=0, tiled=True)]
    dot_general x3 -> x0, matrix products: 107 us -> none  [the longest x1 35.7 us: local_step(): lax.dot_general(grad_z, w_out, (((1,), (1,)), ((), ())), preferred_elemen...]
    psum x1 -> x0, waiting for transfers between devices: 100 us -> none  [local_step(): lax.psum(grad_part.astype(jnp.float32), 'tp').reshape(2, rows, d_model)]
    psum x3 -> x0, blocking collectives: 79.9 us -> none  [the longest x1 29 us: local_step(): lax.psum(jnp.stack([jnp.sum(shifted, axis=-1), jnp.sum(jnp.where(is_targe...]
    pmax x1 -> x0, blocking collectives: 35.5 us -> none  [local_step(): row_max = lax.pmax(jnp.max(logits, axis=-1), 'tp')]
    convert_element_type x3 -> x0, other arithmetic: 27.9 us -> none  [the longest x1 18.3 us: local_step(): (row_w[:, None] * jnp.where(is_target, soft_probs - 1.0, soft_probs)).ast...]
    reduce_sum x6 -> x0, other arithmetic: 19.7 us -> none  [the longest x1 10.4 us: local_step(): jnp.sum(shifted, axis=-1)]
  transfers between devices with their start and end apart: 2 -> 0, of which waited for: 2 -> 0; matrix products, arithmetic and copies ran while one was open for 10% -> 0% of each run, Pallas kernels for 0% -> 0%
where the time goes in v3:
time: 240 us; the launch traced here: 239 us
  Pallas kernels  238 us (99%)
    pallas_call x1, Pallas kernels, head_grad(): pl.pallas_call(head_kernel, out_shape=(shape((2, half, FEATS), F32), shap...  160 us
    pallas_call x1, Pallas kernels, logits(): pl.pallas_call(logits_kernel, out_shape=(shape((rows, vocab), F32), shape...  67.1 us
    pallas_call x1, Pallas kernels, finish(): pl.pallas_call(finish_kernel, out_shape=(shape((block, 2 * half), F32), s...  11.1 us

profile of v3, /device:TPU:1, one launch (start us, length us, event | category | flops | bytes accessed | tf_op | source)
XLA Modules:
  0.0 238.9 jit_solution(2692287698547928838)
XLA Ops:
  0.6 67.1 %logits.1 = (f32[1024,6400]{1,0:T(8,128)}, bf16[1024,2048]{1,0:T(8,128)(2,1)}, bf16[1024,2048]{1,0:T(8,128)(2,1)}, f32[1024,2048]{1,0:T(8,128)}, f32[1024,2048]{...) custom-call(bf16[512,2048]{1,0:T(8,128)(2,1)} %bitcast.9, bf16[512,2048]{1,0:T(8,128)(2,1)} %bitcast.11, ...), custom_call_target="tpu_custom_call" | custom-call | tf_op jit(solution)/shard_map/logits/pallas_call | solution.py:387
  67.7 159.8 %head_grad.1 = (f32[2,3200,256]{2,1,0:T(8,128)}, f32[1024,2048]{1,0:T(8,128)}, bf16[512,2048]{1,0:T(8,128)(2,1)}, f32[1024,2048]{1,0:T(8,128)}, f32[1024,2048]{1...) custom-call(bf16[512,2048]{1,0:T(8,128)(2,1)} %bitcast.10, ...), custom_call_target="tpu_custom_call", output_to_operand_aliasing={{4}: (6, {})} | custom-call | tf_op jit(solution)/shard_map/head_grad/pallas_call | solution.py:800
  227.6 11.1 %finish.1 = (f32[256,6400]{1,0:T(8,128)}, bf16[512,2048]{1,0:T(8,128)(2,1)}, bf16[512,2048]{1,0:T(8,128)(2,1)}, f32[1,1]{1,0:T(1,128)}, f32[1,2048]{1,0:T(1,128)}, /*index=5*/f32[1,2048]{1,0:T(1,128)}) custom-call(f32[2,3200,256]{2,1,0:T(8,128)} %get-tuple-element.30.fin, f32[1024,2048]{1,0:T(8,128)} %get-tuple-element.31.gh, ...), custom_call_target="tpu_custom_call" | custom-call | tf_op jit(solution)/shard_map/finish/pallas_call | solution.py:861

commit v4 on v3

--- a/solution.py
+++ b/solution.py
@@ -27,11 +27,11 @@
 SPREAD = 2 * RING * RING * SLICE
 FIRST, WIDE = 128, 384
 TASK = 512
-KINDS = "nnnnnsnsn"
-DONE = (0, 5, 8, 16) + 5 * (20,)
-ACTS = ("1a:f2,a1", "2t:L0", "3t:f3", "4t:C0", "2a:a2", "2d:L1,r00,u0", "3m:f4", "9t:a3,C1", "13t:L2,r01", "14t:C2", "3d:f5,r10,u1",
-        "4m:r02", "18t:L3,a4", "19t:C3,r03", "4d:r11", "5m:r04", "5a:a5", "6m:r12,r05", "6a:a6", "7m:r13,r06", "7a:a7,r14,L4,g0")
-TAIL = ("a8,C4,L5,r15,g1,C5,L6,C6,r16,r07,p70,q70,p71,q71,p80,q80", "p81,q81,r17,g2,r08,n,r18,z")
+KINDS = "nnnnnnnsn"
+DONE = (0, 5, 8, 14, 16) + 4 * (20,)
+ACTS = ("1m:f2", "1a:a1", "1t:f3", "2t:L0", "4t:C0", "2a:a2", "2d:r00,u0,L1", "3m:C1", "8t:a3", "9t:r01", "13t:f4", "4m:r02,L2", "4a:C2",
+        "14t:a4", "4d:r03,f5,r10", "5m:r04,u1,L3", "5a:a5,C3", "5d:r05,r11", "6m:L4", "6a:a6,C4,r06", "7m:r12", "7a:a7", "8m:L5", "8a:a8,C5,r13")
+TAIL = ("r14,g0,r15,r07,g1,r16,L7,C7,L6,C6,p80,q80,r08", "r17,p81,q81,n,g2,r18,z")
 
 
 def ds(start, size, unit=8):
@@ -729,7 +729,6 @@
         u_wait(0)
 
     def before_sends():
-        spread_stats(2)
         u_wait(1)
         with jax.named_scope("meet"):
             met()
@@ -738,6 +737,7 @@
     with jax.named_scope("make0"):
         make(0, 0, more_loads, before_other, before_sends)
     add(0)
+    spread_stats(2)
 
     @pl.loop(1, last + 1)
     def _(k):

time: 240 us -> 234 us (0.975)
  Pallas kernels: 238 us -> 232 us
    pallas_call x1, Pallas kernels: 160 us -> 154 us  [head_grad(): pl.pallas_call(head_kernel, out_shape=(shape((2, half, FEATS), F32), shap...]
where the time goes in v4:
time: 234 us; the launch traced here: 233 us
  Pallas kernels  232 us (99%)
    pallas_call x1, Pallas kernels, head_grad(): pl.pallas_call(head_kernel, out_shape=(shape((2, half, FEATS), F32), shap...  154 us
    pallas_call x1, Pallas kernels, logits(): pl.pallas_call(logits_kernel, out_shape=(shape((rows, vocab), F32), shape...  67.1 us
    pallas_call x1, Pallas kernels, finish(): pl.pallas_call(finish_kernel, out_shape=(shape((block, 2 * half), F32), s...  11.1 us

profile of v4, /device:TPU:1, one launch (start us, length us, event | category | flops | bytes accessed | tf_op | source)
XLA Modules:
  0.0 233.0 jit_solution(14602890457012655908)
XLA Ops:
  0.6 67.1 %logits.1 = (f32[1024,6400]{1,0:T(8,128)}, bf16[1024,2048]{1,0:T(8,128)(2,1)}, bf16[1024,2048]{1,0:T(8,128)(2,1)}, f32[1024,2048]{1,0:T(8,128)}, f32[1024,2048]{...) custom-call(bf16[512,2048]{1,0:T(8,128)(2,1)} %bitcast.9, bf16[512,2048]{1,0:T(8,128)(2,1)} %bitcast.11, ...), custom_call_target="tpu_custom_call" | custom-call | tf_op jit(solution)/shard_map/logits/pallas_call | solution.py:387
  67.7 154.0 %head_grad.1 = (f32[2,3200,256]{2,1,0:T(8,128)}, f32[1024,2048]{1,0:T(8,128)}, bf16[512,2048]{1,0:T(8,128)(2,1)}, f32[1024,2048]{1,0:T(8,128)}, f32[1024,2048]{1...) custom-call(bf16[512,2048]{1,0:T(8,128)(2,1)} %bitcast.10, ...), custom_call_target="tpu_custom_call", output_to_operand_aliasing={{4}: (6, {})} | custom-call | tf_op jit(solution)/shard_map/head_grad/pallas_call | solution.py:800
  221.7 11.1 %finish.1 = (f32[256,6400]{1,0:T(8,128)}, bf16[512,2048]{1,0:T(8,128)(2,1)}, bf16[512,2048]{1,0:T(8,128)(2,1)}, f32[1,1]{1,0:T(1,128)}, f32[1,2048]{1,0:T(1,128)}, /*index=5*/f32[1,2048]{1,0:T(1,128)}) custom-call(f32[2,3200,256]{2,1,0:T(8,128)} %get-tuple-element.30.fin, f32[1024,2048]{1,0:T(8,128)} %get-tuple-element.31.gh, ...), custom_call_target="tpu_custom_call" | custom-call | tf_op jit(solution)/shard_map/finish/pallas_call | solution.py:861

commit v5 on v4

--- a/solution.py
+++ b/solution.py
@@ -31,7 +31,7 @@
 DONE = (0, 5, 8, 14, 16) + 4 * (20,)
 ACTS = ("1m:f2", "1a:a1", "1t:f3", "2t:L0", "4t:C0", "2a:a2", "2d:r00,u0,L1", "3m:C1", "8t:a3", "9t:r01", "13t:f4", "4m:r02,L2", "4a:C2",
         "14t:a4", "4d:r03,f5,r10", "5m:r04,u1,L3", "5a:a5,C3", "5d:r05,r11", "6m:L4", "6a:a6,C4,r06", "7m:r12", "7a:a7", "8m:L5", "8a:a8,C5,r13")
-TAIL = ("r14,g0,r15,r07,g1,r16,L7,C7,L6,C6,p80,q80,r08", "r17,p81,q81,n,g2,r18,z")
+TAIL = ("r14,g0,r15,r07,g1,r16,L7,C7,L6,C6,p80,q80,r08", "r17,p81,q81,n0,g2,r18,n1,z")
 
 
 def ds(start, size, unit=8):
@@ -540,13 +540,12 @@
     def o_copy(k):
         return near(sum_v.at[span(k), ds(x * FEATS, FEATS, FEATS)], fin.at[0, span(k), :], sem_o)
 
-    def make(k, slot, early=lambda: None, late=lambda: None, middle=lambda: None):
+    def make(k, slot, late=lambda: None, middle=lambda: None):
         width = span(k).size
         swapped = pick(swaps, k)
         col = column(here, used, swapped, 0, pick(offsets, k)).astype(F32)
         arrived(w_v.at[slot, :, upto(width)], sem_w.at[slot])
         arrived(z_v.at[slot, :, upto(width)], sem_z.at[slot])
-        early()
 
         def put(zz, r, c, at):
             e = grad_logits(zz, lse_v[r, :], rw_v[r, :], lab_v[r, :], col + c)
@@ -667,13 +666,13 @@
         if stage == 2:
             tot[:] = functools.reduce(jnp.add, line.blocks())
 
-    def narrow():
-        r = upto(seq)
+    def narrow(h):
+        r = ds(h * seq, seq)
         c = near(gh.at[r, :], acc_v, sem_a)
         c.start()
         c.wait()
         u_v[r, :] = acc_v[:].astype(BF16)
-        near(u_v.at[r, :], ghb, sem_a).start()
+        near(u_v.at[r, :], ghb.at[r, :], sem_x.at[h]).start()
 
     far_steps = [plane_gather(here, far_u, s, gs, gr) for s in BOTH]
 
@@ -719,25 +718,23 @@
 
     spread_stats(1)
 
-    def more_loads():
-        begin(u_copies(1))
-        fetch(1, 1)
-        begin(acc_copies(0, False))
-
     def before_other():
         spread_stats(0)
         u_wait(0)
+        begin(u_copies(1))
 
     def before_sends():
         u_wait(1)
+        fetch(1, 1)
+        begin(acc_copies(0, False))
         with jax.named_scope("meet"):
             met()
         far_event(1)
 
     with jax.named_scope("make0"):
-        make(0, 0, more_loads, before_other, before_sends)
+        make(0, 0, before_other, before_sends)
+    spread_stats(2)
     add(0)
-    spread_stats(2)
 
     @pl.loop(1, last + 1)
     def _(k):
@@ -786,7 +783,8 @@
         arrived(fin.at[1], f_send)
         arrived(fin.at[1], f_recv)
         arrived(fin.at[0], sem_o)
-        arrived(ghb, sem_a)
+        for h in BOTH:
+            arrived(ghb.at[upto(seq), :], sem_x.at[h])
 
 
 def head_grad(hm, ht, gain_m, gain_t, u_own, u_par, far_u, z, w, st, du_in, lpart):
@@ -799,7 +797,7 @@
     stat = pltpu.VMEM((3 * rows, LANES), F32)
     return pl.pallas_call(
         head_kernel,
-        out_shape=(shape((2, half, FEATS), F32), shape((rows, depth), F32), shape((seq, depth), BF16), shape((rows, depth), F32),
+        out_shape=(shape((2, half, FEATS), F32), shape((rows, depth), F32), shape((rows, depth), BF16), shape((rows, depth), F32),
                    shape((rows, depth), F32), shape((2, half, FEATS), F32), shape((4, depth), F32)),
         in_specs=[ANY, ANY, VMEM, VMEM] + [ANY] * 5 + [VMEM, ANY, VMEM],
         out_specs=(ANY,) * 6 + (VMEM,),
@@ -821,7 +819,7 @@
     )(hm, ht, gain_m, gain_t, u_own, u_par, far_u, z, w, st, du_in, lpart)
 
 
-def finish_kernel(fin, gh, ghb, tot, out, gm, gt, loss, ggm, ggt, f_v, o_v, g_v, m_v, t_v, sem_f, sem_o, sem_g):
+def finish_kernel(fin, gh, tot, out, gm, gt, loss, ggm, ggt, f_v, o_v, g_v, sem_f, sem_o, sem_g):
     seq = gm.shape[0]
     table, used = chunk_table()
     jobs = [(k, *t) for t in table for k in BOTH]
@@ -835,47 +833,43 @@
         k, at, width, swapped, offset = jobs[i]
         return near(o_v.at[k, :, pl.ds(at, width)], out.at[:, ds(column(here, used, swapped, k, offset), width, LANES)], sem_o.at[i])
 
-    g_in, m_in = near(gh.at[pl.ds(seq, seq), :], g_v, sem_g.at[0]), near(ghb, m_v, sem_g.at[1])
+    g_in = [near(gh.at[pl.ds(h * seq, seq), :], g_v.at[h], sem_g.at[h]) for h in BOTH]
     begin([f_in(i) for i in range(WINDOW)])
     ggm[:], ggt[:], loss[:] = tot[0:1, :], tot[1:2, :], tot[2:3, 0:1]
-    outs = [f_out(i) for i in range(len(jobs))] + [near(t_v, gt, sem_g.at[0]), near(m_v, gm, sem_g.at[1])]
+    outs = [f_out(i) for i in range(len(jobs))] + [near(g_v.at[h], (gm, gt)[h], sem_g.at[h]) for h in BOTH]
     for i, (k, at, width, _, _) in enumerate(jobs):
-        begin([f_in(i + WINDOW)] if i + WINDOW < len(jobs) else [(m_in, g_in)[i % 2]] if i + 2 >= len(jobs) else [])
+        begin([f_in(i + WINDOW)] if i + WINDOW < len(jobs) else [g_in[i % 2]] if i + 2 >= len(jobs) else [])
         f_in(i).wait()
         o_v[k, :, pl.ds(at, width)] = f_v[k, pl.ds(at, width), :].T
         outs[i].start()
-    m_in.wait()
-    outs[-1].start()
-    g_in.wait()
-    t_v[:] = g_v[:].astype(BF16)
-    outs[-2].start()
+    for h in BOTH:
+        g_in[h].wait()
+        outs[h - 2].start()
     for c in outs:
         c.wait()
 
 
-def finish(fin, gh, ghb, tot):
+def finish(fin, gh, tot):
     _, half, block = fin.shape
-    seq, depth = ghb.shape
+    seq, depth = gh.shape[0] // 2, gh.shape[1]
     shape, row, jobs = jax.ShapeDtypeStruct, jax.ShapeDtypeStruct((1, depth), F32), DMA((2 * len(KINDS),))
-    rows = pltpu.VMEM((seq, depth), BF16)
     return pl.pallas_call(
         finish_kernel,
         out_shape=(shape((block, 2 * half), F32), shape((seq, depth), BF16), shape((seq, depth), BF16), shape((1, 1), F32), row, row),
-        in_specs=[ANY, ANY, ANY, VMEM],
+        in_specs=[ANY, ANY, VMEM],
         out_specs=(ANY, ANY, ANY, VMEM, VMEM, VMEM),
-        scratch_shapes=[pltpu.VMEM((2, half, block), F32), pltpu.VMEM((2, block, half), F32), pltpu.VMEM((seq, depth), F32), rows, rows,
-                        jobs, jobs, TWO],
+        scratch_shapes=[pltpu.VMEM((2, half, block), F32), pltpu.VMEM((2, block, half), F32), pltpu.VMEM((2, seq, depth), BF16), jobs, jobs, TWO],
         compiler_params=pltpu.CompilerParams(vmem_limit_bytes=VMEM_LIMIT),
         name="finish",
-    )(fin, gh, ghb, tot)
+    )(fin, gh, tot)
 
 
 def solution(mesh):
     def local_step(h_main, h_mtp, labels_main, labels_mtp, weight_main, weight_mtp, gain_final, gain_mtp, w_out):
         hm, ht, gm, gt = h_main[0], h_mtp[0], gain_final[None], gain_mtp[None]
         z, u_own, u_par, far_u, du_in, st, lpart = logits(hm, ht, gm, gt, labels_main, labels_mtp, weight_main, weight_mtp, w_out)
-        fin, gh, ghb, _, _, _, tot = head_grad(hm, ht, gm, gt, u_own, u_par, far_u, z, w_out, st, du_in, lpart)
-        grad_w, gh_m, gh_t, loss, gg_m, gg_t = finish(fin, gh, ghb, tot)
+        fin, _, gh, _, _, _, tot = head_grad(hm, ht, gm, gt, u_own, u_par, far_u, z, w_out, st, du_in, lpart)
+        grad_w, gh_m, gh_t, loss, gg_m, gg_t = finish(fin, gh, tot)
         return loss[0, 0], gh_m[None], gh_t[None], grad_w, gg_m[0], gg_t[0]
 
     wide, row = P("dp", None, None), P("dp", None)

time: 234 us -> 232 us (level)
  no operation moved by 1% of the time
where the time goes in v5:
time: 232 us; the launch traced here: 231 us
  Pallas kernels  230 us (99%)
    pallas_call x1, Pallas kernels, head_grad(): pl.pallas_call(head_kernel, out_shape=(shape((2, half, FEATS), F32), shap...  153 us
    pallas_call x1, Pallas kernels, logits(): pl.pallas_call(logits_kernel, out_shape=(shape((rows, vocab), F32), shape...  67.1 us
    pallas_call x1, Pallas kernels, finish(): pl.pallas_call(finish_kernel, out_shape=(shape((block, 2 * half), F32), s...  9.99 us

profile of v5, /device:TPU:1, one launch (start us, length us, event | category | flops | bytes accessed | tf_op | source)
XLA Modules:
  0.0 230.9 jit_solution(8348365139661690890)
XLA Ops:
  0.6 67.1 %logits.1 = (f32[1024,6400]{1,0:T(8,128)}, bf16[1024,2048]{1,0:T(8,128)(2,1)}, bf16[1024,2048]{1,0:T(8,128)(2,1)}, f32[1024,2048]{1,0:T(8,128)}, f32[1024,2048]{...) custom-call(bf16[512,2048]{1,0:T(8,128)(2,1)} %bitcast.9, bf16[512,2048]{1,0:T(8,128)(2,1)} %bitcast.11, ...), custom_call_target="tpu_custom_call" | custom-call | tf_op jit(solution)/shard_map/logits/pallas_call | solution.py:387
  67.7 153.0 %head_grad.1 = (f32[2,3200,256]{2,1,0:T(8,128)}, f32[1024,2048]{1,0:T(8,128)}, bf16[1024,2048]{1,0:T(8,128)(2,1)}, f32[1024,2048]{1,0:T(8,128)}, f32[1024,2048]{...) custom-call(bf16[512,2048]{1,0:T(8,128)(2,1)} %bitcast.10, ...), custom_call_target="tpu_custom_call", output_to_operand_aliasing={{4}: (6, {})} | custom-call | tf_op jit(solution)/shard_map/head_grad/pallas_call | solution.py:798
  220.7 10.0 %finish.1 = (f32[256,6400]{1,0:T(8,128)}, bf16[512,2048]{1,0:T(8,128)(2,1)}, bf16[512,2048]{1,0:T(8,128)(2,1)}, f32[1,1]{1,0:T(1,128)}, f32[1,2048]{1,0:T(1,128)}, /*index=5*/f32[1,2048]{1,0:T(1,128)}) custom-call(f32[2,3200,256]{2,1,0:T(8,128)} %get-tuple-element.29.fin, bf16[1024,2048]{1,0:T(8,128)(2,1)} %get-tuple-element.30.gh, ...), custom_call_target="tpu_custom_call" | custom-call | tf_op jit(solution)/shard_map/finish/pallas_call | solution.py:856

commit v6 on v5

--- a/solution.py
+++ b/solution.py
@@ -15,7 +15,7 @@
 ANY = pl.BlockSpec(memory_space=pl.ANY)
 VMEM = pl.BlockSpec(memory_space=pltpu.VMEM)
 VMEM_LIMIT = 67043328
-WINDOW = 9
+WINDOW = 17
 LANES, FEATS = 128, 256
 RING = 4
 WAYS = (1, -1)
@@ -834,17 +834,17 @@
         return near(o_v.at[k, :, pl.ds(at, width)], out.at[:, ds(column(here, used, swapped, k, offset), width, LANES)], sem_o.at[i])
 
     g_in = [near(gh.at[pl.ds(h * seq, seq), :], g_v.at[h], sem_g.at[h]) for h in BOTH]
-    begin([f_in(i) for i in range(WINDOW)])
+    begin(g_in + [f_in(i) for i in range(WINDOW)])
     ggm[:], ggt[:], loss[:] = tot[0:1, :], tot[1:2, :], tot[2:3, 0:1]
     outs = [f_out(i) for i in range(len(jobs))] + [near(g_v.at[h], (gm, gt)[h], sem_g.at[h]) for h in BOTH]
     for i, (k, at, width, _, _) in enumerate(jobs):
-        begin([f_in(i + WINDOW)] if i + WINDOW < len(jobs) else [g_in[i % 2]] if i + 2 >= len(jobs) else [])
+        begin([f_in(i + WINDOW)] if i + WINDOW < len(jobs) else [])
+        if i < 2:
+            g_in[i].wait()
+            outs[i - 2].start()
         f_in(i).wait()
         o_v[k, :, pl.ds(at, width)] = f_v[k, pl.ds(at, width), :].T
         outs[i].start()
-    for h in BOTH:
-        g_in[h].wait()
-        outs[h - 2].start()
     for c in outs:
         c.wait()
 

time: 232 us -> 231 us (level)
  no operation moved by 1% of the time
where the time goes in v6:
time: 231 us; the launch traced here: 230 us
  Pallas kernels  229 us (99%)
    pallas_call x1, Pallas kernels, head_grad(): pl.pallas_call(head_kernel, out_shape=(shape((2, half, FEATS), F32), shap...  153 us
    pallas_call x1, Pallas kernels, logits(): pl.pallas_call(logits_kernel, out_shape=(shape((rows, vocab), F32), shape...  67.1 us
    pallas_call x1, Pallas kernels, finish(): pl.pallas_call(finish_kernel, out_shape=(shape((block, 2 * half), F32), s...  9.37 us

profile of v6, /device:TPU:1, one launch (start us, length us, event | category | flops | bytes accessed | tf_op | source)
XLA Modules:
  0.0 230.3 jit_solution(4138874392603722070)
XLA Ops:
  0.6 67.1 %logits.1 = (f32[1024,6400]{1,0:T(8,128)}, bf16[1024,2048]{1,0:T(8,128)(2,1)}, bf16[1024,2048]{1,0:T(8,128)(2,1)}, f32[1024,2048]{1,0:T(8,128)}, f32[1024,2048]{...) custom-call(bf16[512,2048]{1,0:T(8,128)(2,1)} %bitcast.9, bf16[512,2048]{1,0:T(8,128)(2,1)} %bitcast.11, ...), custom_call_target="tpu_custom_call" | custom-call | tf_op jit(solution)/shard_map/logits/pallas_call | solution.py:387
  67.7 153.0 %head_grad.1 = (f32[2,3200,256]{2,1,0:T(8,128)}, f32[1024,2048]{1,0:T(8,128)}, bf16[1024,2048]{1,0:T(8,128)(2,1)}, f32[1024,2048]{1,0:T(8,128)}, f32[1024,2048]{...) custom-call(bf16[512,2048]{1,0:T(8,128)(2,1)} %bitcast.10, ...), custom_call_target="tpu_custom_call", output_to_operand_aliasing={{4}: (6, {})} | custom-call | tf_op jit(solution)/shard_map/head_grad/pallas_call | solution.py:798
  220.7 9.4 %finish.1 = (f32[256,6400]{1,0:T(8,128)}, bf16[512,2048]{1,0:T(8,128)(2,1)}, bf16[512,2048]{1,0:T(8,128)(2,1)}, f32[1,1]{1,0:T(1,128)}, f32[1,2048]{1,0:T(1,128)}, /*index=5*/f32[1,2048]{1,0:T(1,128)}) custom-call(f32[2,3200,256]{2,1,0:T(8,128)} %get-tuple-element.29.fin, bf16[1024,2048]{1,0:T(8,128)(2,1)} %get-tuple-element.30.gh, ...), custom_call_target="tpu_custom_call" | custom-call | tf_op jit(solution)/shard_map/finish/pallas_call | solution.py:856
